TPU v7x, 32 devices: a whole 2x2x4 slice. The times are simulated.
32 devices in a mesh: gx: 4 (over y, core), gy: 8 (over z, x).
Axes of the slice: x: 2, y: 2, z: 4, core: 2. Of those that a mesh axis runs over, the one named last changes fastest.
Arguments:
- species: float32 [9, 32, 64, 128], P(None, 'gx', 'gy'), may hold values from -4 to 4
- flow_fields: float32 [5, 32, 64, 128], P(None, 'gx', 'gy'), may hold values from -5 to 5
- classes: int32 [32, 64], P('gx', 'gy'), may hold values from 1 to 4, as said below
- diffusivity: float32 [14], replicated, may hold values from 0.2 to 0.6
- left_form: float32 [19, 9], replicated, may hold values from -2 to 2
- right_form: float32 [19, 9], replicated, may hold values from -2 to 2
- stoich: float32 [19, 9], replicated, may hold values from -1.25 to 1.25
- heat_release: float32 [19], replicated, may hold values from -3 to 3
- arrhenius_prefactor: float32 [19], replicated, may hold values from 0.4 to 4
- arrhenius_energy: float32 [19], replicated, may hold values from 0.5 to 2
- newton_matrix: float32 [10, 10], replicated, may hold values from -0.5 to 1.5
Outputs:
- species_out: float32 [9, 32, 64, 128], P(None, 'gx', 'gy')
- flow_out: float32 [5, 32, 64, 128], P(None, 'gx', 'gy')
Inputs may be any that keep to these rules, and one draw needn't show every extreme that they name: `classes`: 1 where a column takes one substep, 2 to 4 otherwise. Among the columns of one device at most 32 have a class over 1, and some device has exactly that many; two devices with the same gx index whose gy indices differ by half the gy axis hold at most 40 such columns together, and some pair has exactly that many.
All inputs are finite; a program needn't handle non-finite values.
Results may differ from a plain program's by a relative error of at most 0.0003.
Values sent between devices are 32-bit elements; how exact they have to be, the bound alone decides.
A program may use at most 64 MiB of HBM per device.

v0:
```python
import functools

import jax
import jax.numpy as jnp
import ml_dtypes
import numpy as np
from jax import lax
from jax.experimental import pallas as pl
from jax.experimental.pallas import tpu as pltpu
from jax.sharding import PartitionSpec as P

TIME_STEP = 0.25
PRECISE = lax.Precision.HIGHEST


def extended(value, sides, width):
    for axis, dim in sides:
        size, length = (lax.axis_size(axis), value.shape[dim])
        up = [(i, (i + 1) % size) for i in range(size)]
        down = [(j, i) for i, j in up]
        last = lax.slice_in_dim(value, length - width, length, axis=dim)
        first = lax.slice_in_dim(value, 0, width, axis=dim)
        before = lax.ppermute(last, axis, up)
        after = lax.ppermute(first, axis, down)
        value = jnp.concatenate([before, value, after], axis=dim)
    return value


def reaction_rates(burning_mixture_status, params):
    left_form, right_form, stoich, heat_release, arrhenius_prefactor, arrhenius_energy = params
    fractions = burning_mixture_status[:-1]
    thermal_kelvin_field = burning_mixture_status[-1]
    left_sum = jnp.tanh(jnp.einsum("rs,scn->rcn", left_form, fractions, precision=PRECISE))
    right_sum = jnp.tanh(jnp.einsum("rs,scn->rcn", right_form, fractions, precision=PRECISE))
    flow_speed_norm = arrhenius_prefactor[:, None, None] * jax.nn.sigmoid(
        arrhenius_energy[:, None, None] * thermal_kelvin_field[None]
    )
    progress = flow_speed_norm * left_sum * right_sum
    species_rate = jnp.einsum("rs,rcn->scn", stoich, progress, precision=PRECISE)
    heat_rate = jnp.einsum("r,rcn->cn", heat_release, progress, precision=PRECISE)
    return jnp.concatenate([species_rate, heat_rate[None]], axis=0)


def substep(start, step_size, newton_matrix, params):
    current = start
    for repeat in range(3):
        residue = current - start - step_size[None] * reaction_rates(current, params)
        current = current - jnp.einsum("ij,jcn->icn", newton_matrix, residue, precision=PRECISE)
    return current


def extras(buffer, class_value, newton_matrix, params):
    step_size = (TIME_STEP / class_value)[:, None]
    for section in (1, 2, 3):
        active = (class_value > section)[None, :, None]
        buffer = jnp.where(active, substep(buffer, step_size, newton_matrix, params), buffer)
    return buffer


def tables(length):
    index = jnp.arange(length, dtype=jnp.int32)
    phase = index[:, None] * index[None, :] % length
    angle = phase.astype(jnp.float32) * (2.0 * jnp.pi / length)
    return (jnp.cos(angle), jnp.sin(angle))


def half_angles(length):
    index = jnp.arange(length, dtype=jnp.int32)
    modes = jnp.arange(length // 2, dtype=jnp.int32)
    phase = index[:, None] * modes[None, :] % length
    angle = phase.astype(jnp.float32) * (2.0 * jnp.pi / length)
    alternate = jnp.where(index % 2 == 0, 1.0, -1.0).astype(jnp.float32)
    return (angle, alternate, modes)


def transform_dim(array, dimension, lookup):
    moved_last = jnp.moveaxis(array, dimension, -1)
    result = jnp.einsum("...j,jk->...k", moved_last, lookup, precision=PRECISE)
    return jnp.moveaxis(result, -1, dimension)


def forward(spectra, dimension):
    length = spectra.shape[dimension]
    cosine, sine_table = tables(length)
    real_part = spectra[:, 0]
    imag_part = spectra[:, 1]
    inner = dimension - 1
    new_real = transform_dim(real_part, inner, cosine) + transform_dim(imag_part, inner, sine_table)
    new_imag = transform_dim(imag_part, inner, cosine) - transform_dim(real_part, inner, sine_table)
    return jnp.stack([new_real, new_imag], axis=1)


def backward(spectra, dimension):
    length = spectra.shape[dimension]
    cosine, sine_table = tables(length)
    real_part = spectra[:, 0]
    imag_part = spectra[:, 1]
    inner = dimension - 1
    new_real = (
        transform_dim(real_part, inner, cosine) - transform_dim(imag_part, inner, sine_table)
    ) / length
    new_imag = (
        transform_dim(imag_part, inner, cosine) + transform_dim(real_part, inner, sine_table)
    ) / length
    return jnp.stack([new_real, new_imag], axis=1)


def forward_packed(values):
    length = values.shape[3]
    angle, alternate, modes = half_angles(length)
    cosine = jnp.cos(angle)
    packed_sine = jnp.where(modes[None, :] == 0, -alternate[:, None], jnp.sin(angle))
    return jnp.stack(
        [transform_dim(values, 3, cosine), -transform_dim(values, 3, packed_sine)], axis=1
    )


def backward_packed(spectra):
    length = 2 * spectra.shape[4]
    angle, alternate, modes = half_angles(length)
    weight = jnp.where(modes == 0, 1.0, 2.0).astype(jnp.float32)
    cos_back = weight[:, None] * jnp.cos(angle.T)
    sin_back = jnp.where(modes[:, None] == 0, -alternate[None, :], 2.0 * jnp.sin(angle.T))
    return (
        transform_dim(spectra[:, 0], 3, cos_back) - transform_dim(spectra[:, 1], 3, sin_back)
    ) / length


def wave_numbers(index, length):
    signed = jnp.where(index < (length + 1) // 2, index, index - length)
    waves = signed.astype(jnp.float32) * (2.0 * jnp.pi / length)
    return jnp.where(index == length // 2, 0.0, waves)


def project(spectra, rows_x, total_x, rows_y, total_y, rows_z, total_z):
    wave_x = wave_numbers(rows_x, total_x)[:, None, None]
    wave_y = wave_numbers(rows_y, total_y)[None, :, None]
    wave_z = wave_numbers(rows_z, total_z)[None, None, :]
    wavenumber_squared = wave_x * wave_x + wave_y * wave_y + wave_z * wave_z
    denom = jnp.where(wavenumber_squared > 0, wavenumber_squared, 1.0)
    vel_real = spectra[:3, 0]
    vel_imag = spectra[:3, 1]
    source_real = spectra[3, 0]
    source_imag = spectra[3, 1]
    inner_product_real = wave_x * vel_real[0] + wave_y * vel_real[1] + wave_z * vel_real[2]
    imaginary_inner_sum = wave_x * vel_imag[0] + wave_y * vel_imag[1] + wave_z * vel_imag[2]
    waves = (wave_x, wave_y, wave_z)
    outputs = []
    for axis in range(3):
        out_real = (
            vel_real[axis]
            - waves[axis] * inner_product_real / denom
            + waves[axis] * source_imag / denom
        )
        out_imag = (
            vel_imag[axis]
            - waves[axis] * imaginary_inner_sum / denom
            - waves[axis] * source_real / denom
        )
        outputs.append(jnp.stack([out_real, out_imag], axis=0))
    return jnp.stack(outputs, axis=0)


def stream_lines(spectra):
    return forward(spectra, 2)


def span_lines(spectra):
    return forward(spectra, 3)


def stream_inverse(spectra):
    return backward(spectra, 2)


def shards(
    species,
    flow_fields,
    classes,
    diffusivity,
    left_form,
    right_form,
    stoich,
    heat_release,
    arrhenius_prefactor,
    arrhenius_energy,
    newton_matrix,
):
    params = (left_form, right_form, stoich, heat_release, arrhenius_prefactor, arrhenius_energy)
    nspec = species.shape[0]
    cells_x, cells_y, depth = (species.shape[1], species.shape[2], species.shape[3])
    total_x = cells_x * lax.axis_size("gx")
    total_y = cells_y * lax.axis_size("gy")
    fields = jnp.concatenate([species, flow_fields], axis=0)
    padded = extended(fields, (("gx", 1), ("gy", 2)), 1)
    ahead_x = padded[:, 2:, 1:-1]
    behind_x = padded[:, :-2, 1:-1]
    ahead_y = padded[:, 1:-1, 2:]
    behind_y = padded[:, 1:-1, :-2]
    ahead_z = jnp.roll(fields, -1, 3)
    behind_z = jnp.roll(fields, 1, 3)
    stream_vel = flow_fields[1][None]
    span_vel = flow_fields[2][None]
    depth_vel = flow_fields[3][None]
    laplace_sum = ahead_x + behind_x + ahead_y + behind_y + ahead_z + behind_z - 6.0 * fields
    advection = 0.5 * (
        stream_vel * (ahead_x - behind_x)
        + span_vel * (ahead_y - behind_y)
        + depth_vel * (ahead_z - behind_z)
    )
    transported = fields + TIME_STEP * (diffusivity[:, None, None, None] * laplace_sum - advection)
    columns = cells_x * cells_y
    burning_mixture_status = jnp.concatenate(
        [transported[:nspec], transported[nspec + 4 : nspec + 5]], axis=0
    ).reshape(nspec + 1, columns, depth)
    class_flat = classes.reshape(columns)
    class_value = class_flat.astype(jnp.float32)
    burning_mixture_status = substep(
        burning_mixture_status, (TIME_STEP / class_value)[:, None], newton_matrix, params
    )
    stiff = class_flat > 1
    ranking = jnp.argsort(jnp.where(stiff, 0, 1).astype(jnp.int32), stable=True)
    stiff_count = jnp.sum(stiff.astype(jnp.int32))
    stiff_cap = columns // 2
    own_slots = ranking[:stiff_cap]
    live_slots = jnp.arange(stiff_cap) < stiff_count
    buffer = burning_mixture_status[:, own_slots]
    holding_category = jnp.where(live_slots, class_value[own_slots], 1.0)
    buffer = extras(buffer, holding_category, newton_matrix, params)
    burning_mixture_status = burning_mixture_status.at[:, own_slots].set(
        jnp.where(live_slots[None, :, None], buffer, burning_mixture_status[:, own_slots])
    )
    reacted = burning_mixture_status.reshape(nspec + 1, cells_x, cells_y, depth)
    source = (reacted[nspec] - transported[nspec + 4]) / TIME_STEP
    inputs = jnp.concatenate([transported[nspec + 1 : nspec + 4], source[None]], axis=0)
    spectra = forward_packed(inputs)
    spectra = stream_lines(lax.all_to_all(spectra, "gx", split_axis=4, concat_axis=2, tiled=True))
    spectra = span_lines(lax.all_to_all(spectra, "gy", split_axis=2, concat_axis=3, tiled=True))
    local_x = spectra.shape[2]
    local_z = spectra.shape[4]
    rows_x = lax.axis_index("gy") * local_x + jnp.arange(local_x, dtype=jnp.int32)
    rows_y = jnp.arange(total_y, dtype=jnp.int32)
    rows_z = lax.axis_index("gx") * local_z + jnp.arange(local_z, dtype=jnp.int32)
    projected = project(spectra, rows_x, total_x, rows_y, total_y, rows_z, depth)
    projected = backward(projected, 3)
    projected = stream_inverse(
        lax.all_to_all(projected, "gy", split_axis=3, concat_axis=2, tiled=True)
    )
    velocity = backward_packed(
        lax.all_to_all(projected, "gx", split_axis=2, concat_axis=4, tiled=True)
    )
    species_out = reacted[:nspec]
    flow_out = jnp.concatenate(
        [transported[nspec : nspec + 1], velocity, reacted[nspec : nspec + 1]], axis=0
    )
    return (species_out, flow_out)


F32 = jnp.float32
BF16 = jnp.bfloat16
SLOT = 16
GROUP = 24
VMEM_BYTES = 16 * 2**20
WIDE_FIRST = 32
WIDE_MORE = 16


def split_constant(array):
    high = array.astype(ml_dtypes.bfloat16)
    low = (array - high.astype(np.float64)).astype(ml_dtypes.bfloat16)
    return high, low


def spectral_constants(grid_x, grid_y, cells_x, cells_y, depth):
    devices = grid_x * grid_y
    modes = depth // 2 // devices
    total_x, total_y = grid_x * cells_x, grid_y * cells_y
    z = np.arange(depth)
    m = np.arange(devices * modes)
    angle = 2 * np.pi * ((m[:, None] * z[None, :]) % depth) / depth
    alternate = np.where(z % 2 == 0, 1.0, -1.0)
    into = np.stack([np.cos(angle), -np.sin(angle)], 1)
    into[0, 1] = alternate
    back = np.stack([2 * np.cos(angle), -2 * np.sin(angle)], 1)
    back[0, 0] = 1.0
    back[0, 1] = alternate
    back = back / (depth * total_x * total_y)
    pair = np.eye(2)

    def depth_matrix(lines):
        lines = lines.reshape(devices, modes, 2, depth)
        full = np.einsum("dmrz,pq->dpmrqz", lines, pair)
        return full.reshape(devices * 4 * modes, 2 * depth)

    gx, gy = np.arange(grid_x), np.arange(grid_y)
    xl, yl = np.arange(cells_x), np.arange(cells_y)
    wave = lambda a, b, n: np.exp(-2j * np.pi * ((a[:, None] * b[None, :]) % n) / n)
    left = np.kron(wave(gx, gx, grid_x), wave(gy, gy, grid_y))
    real = np.stack([np.stack([left.real, -left.imag], -1), np.stack([left.imag, left.real], -1)], -2)
    left = np.einsum("kgrs,pq->kprgqs", real, np.eye(2 * modes)).reshape(4 * modes * devices, -1)
    twist = np.kron(wave(gx, xl, total_x), wave(gy, yl, total_y))
    twist = np.tile(twist, (1, 2))[:, None, :]
    inner = np.kron(wave(xl, xl, cells_x), wave(yl, yl, cells_y))
    right = np.concatenate([np.kron(pair, inner.real), np.kron(pair, inner.imag)], 0)
    right_back = np.concatenate([np.kron(pair, inner.real), -np.kron(pair, inner.imag)], 0)

    def waves(index, length):
        signed = np.where(index < (length + 1) // 2, index, index - length) * (2 * np.pi / length)
        return np.where(index == length // 2, 0.0, signed)

    kx = waves(gx[:, None] + grid_x * xl[None, :], total_x)
    ky = waves(gy[:, None] + grid_y * yl[None, :], total_y)
    shape = (grid_x, grid_y, cells_x, cells_y)
    kx = np.broadcast_to(kx[:, None, :, None], shape).reshape(devices, 1, cells_x * cells_y)
    ky = np.broadcast_to(ky[None, :, None, :], shape).reshape(devices, 1, cells_x * cells_y)
    kxy = np.concatenate([kx, ky], -1)
    square = np.concatenate([kx * kx + ky * ky] * 2, -1)
    parts = []
    for matrix in (depth_matrix(into), left, right, right_back, left.T, depth_matrix(back).T):
        parts.extend(split_constant(np.ascontiguousarray(matrix)))
    parts.extend(np.ascontiguousarray(a, dtype=np.float32) for a in (twist.real, twist.imag, kxy, square))
    return parts


def halves(value):
    high = value.astype(BF16)
    low = (value - high.astype(F32)).astype(BF16)
    return high, low


def mul(a, b):
    return jnp.dot(a, b, preferred_element_type=F32)


def mul_t(a, b):
    return lax.dot_general(a, b, (((1,), (1,)), ((), ())), preferred_element_type=F32)


def dot_left(high_ref, low_ref, value, product=mul):
    high, low = halves(value)
    a, b = high_ref[...], low_ref[...]
    return product(a, high) + product(a, low) + product(b, high)


def dot_right(value, high_ref, low_ref):
    high, low = halves(value)
    a, b = high_ref[...], low_ref[...]
    return mul(high, a) + mul(low, a) + mul(high, b)


def turn(value):
    rows = value.shape[1]
    parity = lax.broadcasted_iota(jnp.int32, value.shape, 1) % 2
    return jnp.where(parity == 0, -pltpu.roll(value, rows - 1, 1), pltpu.roll(value, 1, 1))


def newton(start, step, forms, update):
    state = start
    pad = jnp.zeros((8, start.shape[1]), F32)
    for repeat in range(3):
        high, low = halves(state)
        curves = jnp.tanh(mul(forms, jnp.concatenate([high, low, high], axis=0)))
        rates = (1.0 + curves[2 * GROUP :]) * curves[:GROUP] * curves[GROUP : 2 * GROUP] * step
        high, low = halves(jnp.concatenate([state - start, rates, pad], axis=0))
        state = state + mul(update, jnp.concatenate([high, low, high], axis=0))
    return state


def transport_kernel(
    grid_x, grid_y, diffusivity, species_hbm, flow_hbm, moved,
    fields, edge_lo, edge_hi, halo_x, halo_y, load_sem, halo_send, halo_recv,
):
    gx, gy = lax.axis_index("gx"), lax.axis_index("gy")
    nspec = species_hbm.shape[0]
    nfield = fields.shape[0]
    cells_x, cells_y, depth = fields.shape[1:]
    loads = (
        pltpu.make_async_copy(species_hbm, fields.at[pl.ds(0, nspec)], load_sem.at[0]),
        pltpu.make_async_copy(flow_hbm, fields.at[pl.ds(nspec, nfield - nspec)], load_sem.at[1]),
    )
    for load in loads:
        load.start()
    barrier = pltpu.get_barrier_semaphore()
    up_x = {"gx": lax.rem(gx + 1, grid_x), "gy": gy}
    down_x = {"gx": lax.rem(gx + grid_x - 1, grid_x), "gy": gy}
    up_y = {"gx": gx, "gy": lax.rem(gy + 1, grid_y)}
    down_y = {"gx": gx, "gy": lax.rem(gy + grid_y - 1, grid_y)}
    for device in (up_x, down_x, up_y, down_y):
        pl.semaphore_signal(barrier, inc=1, device_id=device, device_id_type=pl.DeviceIdType.MESH)
    for load in loads:
        load.wait()

    @pl.loop(0, nfield)
    def edges(f):
        for x in range(cells_x):
            edge_lo[f, x] = fields[f, x, 0]
            edge_hi[f, x] = fields[f, x, cells_y - 1]

    pl.semaphore_wait(barrier, 4)
    sends = []
    for at, (source, target, device) in enumerate((
        (fields.at[:, cells_x - 1], halo_x.at[0], up_x),
        (fields.at[:, 0], halo_x.at[1], down_x),
        (edge_hi, halo_y.at[0], up_y),
        (edge_lo, halo_y.at[1], down_y),
    )):
        sends.append(pltpu.make_async_remote_copy(
            src_ref=source, dst_ref=target, send_sem=halo_send.at[at], recv_sem=halo_recv.at[at],
            device_id=device, device_id_type=pl.DeviceIdType.MESH))
        sends[-1].start()
    for send in sends:
        send.wait()

    rows = lax.broadcasted_iota(jnp.int32, (cells_y, depth), 0)

    @pl.loop(0, nfield)
    def transport(f):
        coefficient = diffusivity[f]
        for x in range(cells_x):
            here = fields[f, x]
            ahead_x = fields[f, x + 1] if x + 1 < cells_x else halo_x[1, f]
            behind_x = fields[f, x - 1] if x > 0 else halo_x[0, f]
            ahead_y = jnp.where(rows == cells_y - 1, halo_y[1, f, pl.ds(x, 1)], pltpu.roll(here, cells_y - 1, 0))
            behind_y = jnp.where(rows == 0, halo_y[0, f, pl.ds(x, 1)], pltpu.roll(here, 1, 0))
            ahead_z = pltpu.roll(here, depth - 1, 1)
            behind_z = pltpu.roll(here, 1, 1)
            laplace = ahead_x + behind_x + ahead_y + behind_y + ahead_z + behind_z - 6.0 * here
            advection = 0.5 * (
                fields[nspec + 1, x] * (ahead_x - behind_x)
                + fields[nspec + 2, x] * (ahead_y - behind_y)
                + fields[nspec + 3, x] * (ahead_z - behind_z)
            )
            moved[f, x] = here + TIME_STEP * (coefficient * laplace - advection)


def chemistry_kernel(
    kinds, left_ref, right_ref, stoich_ref, heat_ref, prefactor_ref, energy_ref, newton_ref, moved,
    species_out, hot_out, source_out, state, table, forms_t, update_f, order,
):
    nfield, cells_x, cells_y, depth = moved.shape
    nspec, nreac = left_ref.shape
    columns = cells_x * cells_y

    state[...] = jnp.zeros_like(state)
    for f in range(nspec + 1):
        source = f if f < nspec else nfield - 1
        for x in range(cells_x):
            state[pl.ds(x * cells_y * SLOT + f, cells_y, stride=SLOT), :] = moved[source, x]

    forms_t[...] = jnp.zeros_like(forms_t)
    forms_t[0:nspec, 0:nreac] = left_ref[...]
    forms_t[0:nspec, GROUP : GROUP + nreac] = right_ref[...]
    forms_t[nspec : nspec + 1, 2 * GROUP : 2 * GROUP + nreac] = 0.5 * energy_ref[...]
    base = forms_t[0:SLOT, :]
    high, low = halves(base)
    high, low = high.astype(F32), low.astype(F32)
    forms_t[SLOT : 2 * SLOT, :] = high
    forms_t[2 * SLOT : 3 * SLOT, :] = low
    forms_t[0:SLOT, :] = high
    forms = jnp.transpose(forms_t[...])[: 3 * GROUP, : 3 * SLOT].astype(BF16)

    table[...] = jnp.zeros_like(table)
    table[0:nspec, 0:nreac] = stoich_ref[...] * (0.5 * prefactor_ref[...])
    table[nspec : nspec + 1, 0:nreac] = heat_ref[...] * (0.5 * prefactor_ref[...])
    update_f[...] = jnp.zeros_like(update_f)
    update_f[0 : nspec + 1, 0 : nspec + 1] = newton_ref[...]
    mixed = jnp.dot(update_f[:, 0:depth], table[...], precision=PRECISE, preferred_element_type=F32)
    update_f[:, 0:SLOT] = -update_f[:, 0:SLOT]
    update_f[:, SLOT : SLOT + GROUP] = mixed[:, :GROUP]
    span = SLOT + GROUP + 8
    high, low = halves(update_f[:, 0:span])
    update_f[:, 0:span] = high.astype(F32)
    update_f[:, span : 2 * span] = high.astype(F32)
    update_f[:, 2 * span : 3 * span] = low.astype(F32)
    update = update_f[:, : 3 * span].astype(BF16)

    def kind_of(column):
        return kinds[column // cells_y, lax.rem(column, cells_y)]

    count = jnp.int32(0)
    for level in (4, 3, 2):
        def place(column, count):
            order[count] = column
            return count + jnp.where(kind_of(column) == level, 1, 0)
        count = lax.fori_loop(0, columns, place, count, unroll=8)

    def spread(values):
        return jnp.concatenate([jnp.full((1, depth), v, jnp.int32) for v in values], axis=1).astype(F32)

    def tile(column):
        return pl.ds(pl.multiple_of(column * SLOT, SLOT), SLOT)

    @pl.loop(0, columns // WIDE_FIRST)
    def first(chunk):
        members = [chunk * WIDE_FIRST + j for j in range(WIDE_FIRST)]
        value = jnp.concatenate([state[tile(c), :] for c in members], axis=1)
        value = newton(value, TIME_STEP / spread([kind_of(c) for c in members]), forms, update)
        for j, c in enumerate(members):
            state[tile(c), :] = value[:, j * depth : (j + 1) * depth]

    @pl.loop(0, (count + WIDE_MORE - 1) // WIDE_MORE)
    def more(chunk):
        slots = [chunk * WIDE_MORE + j for j in range(WIDE_MORE)]
        members = [jnp.where(s < count, order[s], columns) for s in slots]
        kind = [jnp.where(s < count, kind_of(jnp.minimum(m, columns - 1)), 1) for s, m in zip(slots, members)]
        value = jnp.concatenate([state[tile(c), :] for c in members], axis=1)
        spans = spread(kind)
        step = TIME_STEP / spans

        def section(at, value):
            return jnp.where(spans > at.astype(F32), newton(value, step, forms, update), value)

        value = lax.fori_loop(1, kind[0], section, value)
        for j, c in enumerate(members):
            state[tile(c), :] = value[:, j * depth : (j + 1) * depth]

    for f in range(nspec):
        for x in range(cells_x):
            species_out[f, x] = state[pl.ds(x * cells_y * SLOT + f, cells_y, stride=SLOT), :]
    for x in range(cells_x):
        hot = state[pl.ds(x * cells_y * SLOT + nspec, cells_y, stride=SLOT), :]
        hot_out[x] = hot
        source_out[x] = (hot - moved[nfield - 1, x]) * (1.0 / TIME_STEP)


def projection_kernel(
    grid_x, grid_y, into_h, into_l, left_h, left_l, right_h, right_l, unright_h, unright_l, unleft_h, unleft_l,
    back_h, back_l, twist_re, twist_im, kxy_ref, square_ref, moved, hot_ref, source_ref,
    flow_out, packed, spectra, unpacked, gathered, out_send, out_recv, back_send, back_recv,
):
    devices = grid_x * grid_y
    gx, gy = lax.axis_index("gx"), lax.axis_index("gy")
    me = gx * grid_y + gy
    nfield, cells_x, cells_y, depth = moved.shape
    nspec = nfield - flow_out.shape[0]
    columns = cells_x * cells_y
    half = 2 * columns
    barrier = pltpu.get_barrier_semaphore()

    def peer(offset):
        other = lax.rem(me + offset, devices)
        return other, {"gx": other // grid_y, "gy": lax.rem(other, grid_y)}

    @pl.loop(1, devices)
    def greet(offset):
        pl.semaphore_signal(barrier, inc=1, device_id=peer(offset)[1], device_id_type=pl.DeviceIdType.MESH)

    first_pair = moved[nspec + 1 : nspec + 3].reshape(half, depth)
    last_pair = jnp.concatenate(
        [moved[nspec + 3].reshape(columns, depth), source_ref[...].reshape(columns, depth)], axis=0)
    lines = jnp.concatenate([first_pair, last_pair], axis=1)
    block = packed.shape[1]
    packed[...] = dot_left(into_h, into_l, lines, mul_t).reshape(packed.shape)
    flow_out[0] = moved[nspec]
    flow_out[4] = hot_ref[...]

    def exchange(source, target, send_sem, recv_sem):
        @pl.loop(1, devices)
        def start(offset):
            other, device = peer(offset)
            pltpu.make_async_remote_copy(
                src_ref=source.at[other], dst_ref=target.at[me],
                send_sem=send_sem.at[other], recv_sem=recv_sem.at[me],
                device_id=device, device_id_type=pl.DeviceIdType.MESH).start()

        target[me] = source[me]

        @pl.loop(1, devices)
        def finish(offset):
            other, device = peer(offset)
            pltpu.make_async_remote_copy(
                src_ref=source.at[other], dst_ref=target.at[other],
                send_sem=send_sem.at[other], recv_sem=recv_sem.at[other],
                device_id=device, device_id_type=pl.DeviceIdType.MESH).wait()

    pl.semaphore_wait(barrier, devices - 1)
    exchange(packed, spectra, out_send, out_recv)

    shape = spectra.shape
    flat = (shape[0] * shape[1], shape[2])
    value = dot_left(left_h, left_l, spectra[...].reshape(flat)).reshape(shape)
    turned = turn(value)
    re, im = twist_re[...], twist_im[...]
    a = value * re + turned * im
    b = turned * re - value * im
    value = dot_right(jnp.concatenate([a.reshape(flat), b.reshape(flat)], axis=1), right_h, right_l).reshape(shape)

    modes = block // 4
    row = lax.broadcasted_iota(jnp.int32, (1,) + shape[1:], 1)
    lane = lax.broadcasted_iota(jnp.int32, (1,) + shape[1:], 2)
    upper = row >= 2 * modes
    second = lane >= columns
    mode = me * modes + lax.rem(row, 2 * modes) // 2
    kz = mode.astype(F32) * (2.0 * np.pi / depth)
    k = jnp.where(upper, jnp.where(second, 0.0, kz), kxy_ref[...])
    square = square_ref[...] + kz * kz
    square = jnp.where(square > 0, square, 1.0)
    total = k * value + jnp.where(jnp.logical_and(upper, second), turn(value), 0.0)
    total = total + pltpu.roll(total, columns, 2)
    total = total + pltpu.roll(total, 2 * modes, 1)
    value = value - k * total / square

    turned = turn(value)
    value = dot_right(
        jnp.concatenate([value.reshape(flat), turned.reshape(flat)], axis=1), unright_h, unright_l).reshape(shape)
    value = value * re - turn(value) * im
    unpacked[...] = dot_left(unleft_h, unleft_l, value.reshape(flat)).reshape(shape)
    exchange(unpacked, gathered, back_send, back_recv)
    result = dot_left_t(jnp.transpose(gathered[...].reshape(flat)), back_h, back_l)
    flow_out[1:3] = result[:, :depth].reshape(2, cells_x, cells_y, depth)
    flow_out[3] = result[:columns, depth:].reshape(cells_x, cells_y, depth)


def dot_left_t(value, high_ref, low_ref):
    high, low = halves(value)
    a, b = high_ref[...], low_ref[...]
    return mul_t(high, a) + mul_t(low, a) + mul_t(high, b)


def flame(
    species, flow_fields, classes, diffusivity, left_form, right_form, stoich, heat_release,
    arrhenius_prefactor, arrhenius_energy, newton_matrix, *constants,
):
    grid_x, grid_y = lax.axis_size("gx"), lax.axis_size("gy")
    nspec, cells_x, cells_y, depth = species.shape
    columns = cells_x * cells_y
    devices = grid_x * grid_y
    block = 2 * depth // devices
    vmem = pl.BlockSpec(memory_space=pltpu.VMEM)
    smem = pl.BlockSpec(memory_space=pltpu.SMEM)
    hbm = pl.BlockSpec(memory_space=pl.ANY)
    nfield = nspec + flow_fields.shape[0]
    box = (devices, block, 2 * columns)
    dma = pltpu.SemaphoreType.DMA
    grid = (cells_x, cells_y, depth)
    shaped = lambda shape: jax.ShapeDtypeStruct(shape, F32)
    moved = pl.pallas_call(
        functools.partial(transport_kernel, grid_x, grid_y),
        out_shape=shaped((nfield,) + grid),
        in_specs=[smem, hbm, hbm],
        out_specs=vmem,
        scratch_shapes=[
            pltpu.VMEM((nfield,) + grid, F32),
            pltpu.VMEM((nfield, cells_x, depth), F32),
            pltpu.VMEM((nfield, cells_x, depth), F32),
            pltpu.VMEM((2, nfield, cells_y, depth), F32),
            pltpu.VMEM((2, nfield, cells_x, depth), F32),
            dma((2,)), dma((4,)), dma((4,)),
        ],
        compiler_params=pltpu.CompilerParams(collective_id=0, has_side_effects=True, vmem_limit_bytes=VMEM_BYTES),
        name="transport",
    )(diffusivity, species, flow_fields)
    line = lambda a: a.reshape(1, -1)
    species_out, hot, source = pl.pallas_call(
        chemistry_kernel,
        out_shape=(shaped(species.shape), shaped(grid), shaped(grid)),
        in_specs=[smem] + [vmem] * 8,
        out_specs=(vmem, vmem, vmem),
        scratch_shapes=[
            pltpu.VMEM(((columns + 1) * SLOT, depth), F32),
            pltpu.VMEM((depth, depth), F32),
            pltpu.VMEM((depth, depth), F32),
            pltpu.VMEM((SLOT, 2 * depth), F32),
            pltpu.SMEM((columns + 1,), jnp.int32),
        ],
        compiler_params=pltpu.CompilerParams(vmem_limit_bytes=VMEM_BYTES),
        name="chemistry",
    )(classes, left_form.T, right_form.T, stoich.T, line(heat_release), line(arrhenius_prefactor),
      line(arrhenius_energy), newton_matrix, moved)
    flow_out = pl.pallas_call(
        functools.partial(projection_kernel, grid_x, grid_y),
        out_shape=shaped(flow_fields.shape),
        in_specs=[vmem] * (len(constants) + 3),
        out_specs=vmem,
        scratch_shapes=[pltpu.VMEM(box, F32)] * 4 + [dma((devices,))] * 4,
        compiler_params=pltpu.CompilerParams(collective_id=1, has_side_effects=True, vmem_limit_bytes=VMEM_BYTES),
        name="projection",
    )(*constants, moved, hot, source)
    return species_out, flow_out


def solution(mesh):
    grid_x, grid_y = mesh.shape["gx"], mesh.shape["gy"]

    def step(species, flow_fields, classes, *rest):
        cells_x = species.shape[1] // grid_x
        cells_y = species.shape[2] // grid_y
        depth = species.shape[3]
        direct = (
            depth == 128 and cells_y == 8 and 2 * cells_x * cells_y == 128
            and depth % (4 * grid_x * grid_y) == 0
        )
        grids = (P(None, "gx", "gy", None), P(None, "gx", "gy", None), P("gx", "gy"))
        constants = ()
        if direct:
            constants = tuple(spectral_constants(grid_x, grid_y, cells_x, cells_y, depth))
        return jax.shard_map(
            flame if direct else shards,
            mesh=mesh,
            in_specs=grids + (P(),) * (len(rest) + len(constants)),
            out_specs=(P(None, "gx", "gy", None), P(None, "gx", "gy", None)),
            check_vma=False,
        )(species, flow_fields, classes, *rest, *constants)

    return step
```

profile of v0, /device:TPU:0, one launch (start us, length us, event | category | flops | bytes accessed | tf_op | source)
XLA Modules:
  0.0 45.4 jit_solution(5134642055639540292)
XLA Ops:
  0.7 0.7 %copy-done.23 = f32[14]{0:T(128)S(1)} copy-done((f32[14]{0:T(128)S(1)}, f32[14]{0:T(128)}, u32[]{:S(2)}) %copy-start.23) | copy-done | bytes 80
  1.3 1.0 %copy-done = f32[9,8,8,128]{3,2,1,0:T(8,128)S(1)} copy-done((f32[9,8,8,128]{3,2,1,0:T(8,128)S(1)}, f32[9,8,8,128]{3,2,1,0:T(8,128)}, u32[]{:S(2)}) %copy-start) | copy-done | bytes 294936
  2.3 0.9 %copy-done.1 = f32[5,8,8,128]{3,2,1,0:T(8,128)S(1)} copy-done((f32[5,8,8,128]{3,2,1,0:T(8,128)S(1)}, f32[5,8,8,128]{3,2,1,0:T(8,128)}, u32[]{:S(2)}) %copy-start.1) | copy-done | bytes 163864
  3.2 0.0 copy-start.24
  3.2 0.0 copy-start.5
  3.2 0.0 copy-start.6
  3.3 0.0 copy-start.7
  3.3 0.0 copy-start.8
  3.3 0.0 copy-start.9
  3.3 0.0 copy-start.11
  3.3 0.0 copy-start.12
  3.3 0.0 copy-start.13
  3.3 0.0 copy-start.16
  3.4 0.0 copy-start.17
  3.4 12.0 %transport.1.moved = f32[14,8,8,128]{3,2,1,0:T(8,128)S(1)} custom-call(f32[14]{0:T(128)S(1)} %copy-done.23, f32[9,8,8,128]{3,2,1,0:T(8,128)S(1)} %copy-done, f32[5,8,8,128]{3,2,1,0:T(8,128)S(1)} %copy-done.1), custom_call_target="tpu_custom_call" | custom-call | tf_op jit(solution)/shard_map/transport/pallas_call | solution.py:637
  15.3 0.0 copy-done.22
  15.3 0.0 copy-done.25
  15.4 0.0 copy-done.26
  15.4 0.0 copy-done.18
  15.4 0.0 copy-done.19
  15.4 0.0 copy-done.20
  15.4 0.0 copy-done.21
  15.4 0.0 copy-done.24
  15.4 0.0 copy-start.2
  15.4 0.0 copy-start.3
  15.4 0.0 copy-start.4
  15.4 0.0 copy-start.10
  15.5 0.0 copy-start.14
  15.5 0.0 copy-start.15
  15.5 9.0 %chemistry.1 = (f32[9,8,8,128]{3,2,1,0:T(8,128)}, f32[8,8,128]{2,1,0:T(8,128)S(1)}, f32[8,8,128]{2,1,0:T(8,128)S(1)}) custom-call(s32[8,8]{1,0:T(8,128)S(1)} %copy-done.22, f32[9,19]{1,0:T(8,128)S(1)} %bitcast.6, f32[9,19]{1,0:T(8,128)S(1)} %bitcast.7, f32[9,19]{1,0:T(8,128)S(1)} %bitcast.8, f32[1,19]{1,0:T(1,128)S(1)} %bitcast.9, f32[1,19]{1,0:T(1,128)S(1)} %bitcast.10, ...), custom_call_target="tpu_custom_call" | custom-call | tf_op jit(solution)/shard_map/chemistry/pallas_call | solution.py:654
  24.6 20.1 %projection.1 = f32[5,8,8,128]{3,2,1,0:T(8,128)S(1)} custom-call(bf16[256,256]{1,0:T(8,128)(2,1)S(1)} %copy-done.2, bf16[256,256]{1,0:T(8,128)(2,1)S(1)} %copy-done.3, bf16[256,256]{1,0:T(8,128)(2,1)S(1)} %copy-done.4, bf16[256,256]{1,0:T(8,128)(2,1)S(1)} %copy-done.5, bf16[256,128]{1,0:T(8,128)(2,1)S(1)} %copy-done.10, bf16[256,128]{1,0:T(8,128)(2,1)S(1)} %copy-done.11, ...), custom_call_target="tpu_custom_call" | custom-call | tf_op jit(solution)/shard_map/projection/pallas_call | solution.py:670
  44.7 0.7 %copy.30 = f32[5,8,8,128]{3,2,1,0:T(8,128)} copy(f32[5,8,8,128]{3,2,1,0:T(8,128)S(1)} %projection.1) | data formatting | bytes 327680
  (26 shorter events, 0.1 us)
Async XLA Ops:
  0.6 14.7 %copy-start.22 = (s32[8,8]{1,0:T(8,128)S(1)}, s32[8,8]{1,0:T(8,128)}, u32[]{:S(2)}) copy-start(s32[8,8]{1,0:T(8,128)} %kinds.1) | copy-start | bytes 772
  0.6 14.7 %copy-start.25 = (f32[19]{0:T(128)S(1)}, f32[19]{0:T(128)}, u32[]{:S(2)}) copy-start(f32[19]{0:T(128)} %param.35) | copy-start | bytes 232
  0.7 14.7 %copy-start.26 = (f32[19]{0:T(128)S(1)}, f32[19]{0:T(128)}, u32[]{:S(2)}) copy-start(f32[19]{0:T(128)} %param.36) | copy-start | bytes 232
  0.7 0.7 %copy-start.23 = (f32[14]{0:T(128)S(1)}, f32[14]{0:T(128)}, u32[]{:S(2)}) copy-start(f32[14]{0:T(128)} %diffusivity.1) | copy-start | bytes 172
  1.3 1.0 %copy-start = (f32[9,8,8,128]{3,2,1,0:T(8,128)S(1)}, f32[9,8,8,128]{3,2,1,0:T(8,128)}, u32[]{:S(2)}) copy-start(f32[9,8,8,128]{3,2,1,0:T(8,128)} %species_hbm.1) | copy-start | bytes 884740
  2.3 0.9 %copy-start.1 = (f32[5,8,8,128]{3,2,1,0:T(8,128)S(1)}, f32[5,8,8,128]{3,2,1,0:T(8,128)}, u32[]{:S(2)}) copy-start(f32[5,8,8,128]{3,2,1,0:T(8,128)} %flow_hbm.1) | copy-start | bytes 491524
  3.2 12.1 %copy-start.18 = (f32[19,9]{0,1:T(8,128)S(1)}, f32[19,9]{0,1:T(8,128)}, u32[]{:S(2)}) copy-start(f32[19,9]{0,1:T(8,128)} %param.31) | copy-start | bytes 2056
  3.2 12.2 %copy-start.19 = (f32[19,9]{0,1:T(8,128)S(1)}, f32[19,9]{0,1:T(8,128)}, u32[]{:S(2)}) copy-start(f32[19,9]{0,1:T(8,128)} %param.32) | copy-start | bytes 2056
  3.2 12.2 %copy-start.20 = (f32[19,9]{0,1:T(8,128)S(1)}, f32[19,9]{0,1:T(8,128)}, u32[]{:S(2)}) copy-start(f32[19,9]{0,1:T(8,128)} %param.33) | copy-start | bytes 2056
  3.2 12.2 %copy-start.21 = (f32[10,10]{1,0:T(8,128)S(1)}, f32[10,10]{1,0:T(8,128)}, u32[]{:S(2)}) copy-start(f32[10,10]{1,0:T(8,128)} %newton_ref.1) | copy-start | bytes 1204
  3.2 12.2 %copy-start.24 = (f32[19]{0:T(128)S(1)}, f32[19]{0:T(128)}, u32[]{:S(2)}) copy-start(f32[19]{0:T(128)} %param.34) | copy-start | bytes 232
  3.2 21.2 %copy-start.5 = (bf16[256,256]{1,0:T(8,128)(2,1)S(1)}, bf16[256,256]{1,0:T(8,128)(2,1)}, u32[]{:S(2)}) copy-start(bf16[256,256]{1,0:T(8,128)(2,1)} %constant.35.clone.left_l) | copy-start | bytes 393220
  3.2 21.2 %copy-start.6 = (bf16[256,256]{1,0:T(8,128)(2,1)S(1)}, bf16[256,256]{1,0:T(8,128)(2,1)}, u32[]{:S(2)}) copy-start(bf16[256,256]{1,0:T(8,128)(2,1)} %constant.40.clone.unleft_h) | copy-start | bytes 393220
  3.3 21.2 %copy-start.7 = (bf16[256,256]{1,0:T(8,128)(2,1)S(1)}, bf16[256,256]{1,0:T(8,128)(2,1)}, u32[]{:S(2)}) copy-start(bf16[256,256]{1,0:T(8,128)(2,1)} %constant.41.clone.unleft_l) | copy-start | bytes 393220
  3.3 21.2 %copy-start.8 = (bf16[256,256]{1,0:T(8,128)(2,1)S(1)}, bf16[256,256]{1,0:T(8,128)(2,1)}, u32[]{:S(2)}) copy-start(bf16[256,256]{1,0:T(8,128)(2,1)} %constant.42.clone.back_h) | copy-start | bytes 393220
  3.3 21.2 %copy-start.9 = (bf16[256,256]{1,0:T(8,128)(2,1)S(1)}, bf16[256,256]{1,0:T(8,128)(2,1)}, u32[]{:S(2)}) copy-start(bf16[256,256]{1,0:T(8,128)(2,1)} %constant.43.clone.back_l) | copy-start | bytes 393220
  3.3 21.2 %copy-start.11 = (bf16[256,128]{1,0:T(8,128)(2,1)S(1)}, bf16[256,128]{1,0:T(8,128)(2,1)}, u32[]{:S(2)}) copy-start(bf16[256,128]{1,0:T(8,128)(2,1)} %constant.37.clone.right_l) | copy-start | bytes 196612
  3.3 21.2 %copy-start.12 = (bf16[256,128]{1,0:T(8,128)(2,1)S(1)}, bf16[256,128]{1,0:T(8,128)(2,1)}, u32[]{:S(2)}) copy-start(bf16[256,128]{1,0:T(8,128)(2,1)} %constant.38.clone.unright_h) | copy-start | bytes 196612
  3.3 21.2 %copy-start.13 = (bf16[256,128]{1,0:T(8,128)(2,1)S(1)}, bf16[256,128]{1,0:T(8,128)(2,1)}, u32[]{:S(2)}) copy-start(bf16[256,128]{1,0:T(8,128)(2,1)} %constant.39.clone.unright_l) | copy-start | bytes 196612
  3.3 21.2 %copy-start.16 = (f32[32,1,128]{2,1,0:T(1,128)S(1)}, f32[32,1,128]{2,1,0:T(1,128)}, u32[]{:S(2)}) copy-start(f32[32,1,128]{2,1,0:T(1,128)} %constant.46.clone.kxy_ref) | copy-start | bytes 49156
  3.4 21.2 %copy-start.17 = (f32[32,1,128]{2,1,0:T(1,128)S(1)}, f32[32,1,128]{2,1,0:T(1,128)}, u32[]{:S(2)}) copy-start(f32[32,1,128]{2,1,0:T(1,128)} %constant.47.clone.square_ref) | copy-start | bytes 49156
  15.4 9.1 %copy-start.2 = (bf16[256,256]{1,0:T(8,128)(2,1)S(1)}, bf16[256,256]{1,0:T(8,128)(2,1)}, u32[]{:S(2)}) copy-start(bf16[256,256]{1,0:T(8,128)(2,1)} %constant.32.clone.into_h) | copy-start | bytes 393220
  15.4 9.1 %copy-start.3 = (bf16[256,256]{1,0:T(8,128)(2,1)S(1)}, bf16[256,256]{1,0:T(8,128)(2,1)}, u32[]{:S(2)}) copy-start(bf16[256,256]{1,0:T(8,128)(2,1)} %constant.33.clone.into_l) | copy-start | bytes 393220
  15.4 9.1 %copy-start.4 = (bf16[256,256]{1,0:T(8,128)(2,1)S(1)}, bf16[256,256]{1,0:T(8,128)(2,1)}, u32[]{:S(2)}) copy-start(bf16[256,256]{1,0:T(8,128)(2,1)} %constant.34.clone.left_h) | copy-start | bytes 393220
  15.4 9.1 %copy-start.10 = (bf16[256,128]{1,0:T(8,128)(2,1)S(1)}, bf16[256,128]{1,0:T(8,128)(2,1)}, u32[]{:S(2)}) copy-start(bf16[256,128]{1,0:T(8,128)(2,1)} %constant.36.clone.right_h) | copy-start | bytes 196612
  15.5 9.1 %copy-start.14 = (f32[32,1,128]{2,1,0:T(1,128)S(1)}, f32[32,1,128]{2,1,0:T(1,128)}, u32[]{:S(2)}) copy-start(f32[32,1,128]{2,1,0:T(1,128)} %constant.44.clone.twist_re) | copy-start | bytes 49156
  15.5 9.1 %copy-start.15 = (f32[32,1,128]{2,1,0:T(1,128)S(1)}, f32[32,1,128]{2,1,0:T(1,128)}, u32[]{:S(2)}) copy-start(f32[32,1,128]{2,1,0:T(1,128)} %constant.45.clone.twist_im) | copy-start | bytes 49156
where the time goes:
time: 44.5 us; the launch traced here: 45.4 us
  Pallas kernels  41 us (92%)
  local copies, waits for them, and re-layouts  3.35 us (8%)
  between operations  0.99 us (2%)
    pallas_call x1, Pallas kernels, flame(): pl.pallas_call(functools.partial(projection_kernel, grid_x, grid_y), out_...  20.1 us
    pallas_call x1, Pallas kernels, flame(): pl.pallas_call(functools.partial(transport_kernel, grid_x, grid_y), out_s...  12 us
    pallas_call x1, Pallas kernels, flame(): pl.pallas_call(chemistry_kernel, out_shape=(shaped(species.shape), shaped...  8.97 us
    unnamed x55, local copies, waits for them, and re-layouts  3.35 us

commit v1 on v0

v1 whole, which is shorter than its diff:
```python
import functools

import jax
import jax.numpy as jnp
import ml_dtypes
import numpy as np
from jax import lax
from jax.experimental import pallas as pl
from jax.experimental.pallas import tpu as pltpu
from jax.sharding import PartitionSpec as P

TIME_STEP = 0.25
PRECISE = lax.Precision.HIGHEST


def extended(value, sides, width):
    for axis, dim in sides:
        size, length = (lax.axis_size(axis), value.shape[dim])
        up = [(i, (i + 1) % size) for i in range(size)]
        down = [(j, i) for i, j in up]
        last = lax.slice_in_dim(value, length - width, length, axis=dim)
        first = lax.slice_in_dim(value, 0, width, axis=dim)
        before = lax.ppermute(last, axis, up)
        after = lax.ppermute(first, axis, down)
        value = jnp.concatenate([before, value, after], axis=dim)
    return value


def reaction_rates(burning_mixture_status, params):
    left_form, right_form, stoich, heat_release, arrhenius_prefactor, arrhenius_energy = params
    fractions = burning_mixture_status[:-1]
    thermal_kelvin_field = burning_mixture_status[-1]
    left_sum = jnp.tanh(jnp.einsum("rs,scn->rcn", left_form, fractions, precision=PRECISE))
    right_sum = jnp.tanh(jnp.einsum("rs,scn->rcn", right_form, fractions, precision=PRECISE))
    flow_speed_norm = arrhenius_prefactor[:, None, None] * jax.nn.sigmoid(
        arrhenius_energy[:, None, None] * thermal_kelvin_field[None]
    )
    progress = flow_speed_norm * left_sum * right_sum
    species_rate = jnp.einsum("rs,rcn->scn", stoich, progress, precision=PRECISE)
    heat_rate = jnp.einsum("r,rcn->cn", heat_release, progress, precision=PRECISE)
    return jnp.concatenate([species_rate, heat_rate[None]], axis=0)


def substep(start, step_size, newton_matrix, params):
    current = start
    for repeat in range(3):
        residue = current - start - step_size[None] * reaction_rates(current, params)
        current = current - jnp.einsum("ij,jcn->icn", newton_matrix, residue, precision=PRECISE)
    return current


def extras(buffer, class_value, newton_matrix, params):
    step_size = (TIME_STEP / class_value)[:, None]
    for section in (1, 2, 3):
        active = (class_value > section)[None, :, None]
        buffer = jnp.where(active, substep(buffer, step_size, newton_matrix, params), buffer)
    return buffer


def tables(length):
    index = jnp.arange(length, dtype=jnp.int32)
    phase = index[:, None] * index[None, :] % length
    angle = phase.astype(jnp.float32) * (2.0 * jnp.pi / length)
    return (jnp.cos(angle), jnp.sin(angle))


def half_angles(length):
    index = jnp.arange(length, dtype=jnp.int32)
    modes = jnp.arange(length // 2, dtype=jnp.int32)
    phase = index[:, None] * modes[None, :] % length
    angle = phase.astype(jnp.float32) * (2.0 * jnp.pi / length)
    alternate = jnp.where(index % 2 == 0, 1.0, -1.0).astype(jnp.float32)
    return (angle, alternate, modes)


def transform_dim(array, dimension, lookup):
    moved_last = jnp.moveaxis(array, dimension, -1)
    result = jnp.einsum("...j,jk->...k", moved_last, lookup, precision=PRECISE)
    return jnp.moveaxis(result, -1, dimension)


def forward(spectra, dimension):
    length = spectra.shape[dimension]
    cosine, sine_table = tables(length)
    real_part = spectra[:, 0]
    imag_part = spectra[:, 1]
    inner = dimension - 1
    new_real = transform_dim(real_part, inner, cosine) + transform_dim(imag_part, inner, sine_table)
    new_imag = transform_dim(imag_part, inner, cosine) - transform_dim(real_part, inner, sine_table)
    return jnp.stack([new_real, new_imag], axis=1)


def backward(spectra, dimension):
    length = spectra.shape[dimension]
    cosine, sine_table = tables(length)
    real_part = spectra[:, 0]
    imag_part = spectra[:, 1]
    inner = dimension - 1
    new_real = (
        transform_dim(real_part, inner, cosine) - transform_dim(imag_part, inner, sine_table)
    ) / length
    new_imag = (
        transform_dim(imag_part, inner, cosine) + transform_dim(real_part, inner, sine_table)
    ) / length
    return jnp.stack([new_real, new_imag], axis=1)


def forward_packed(values):
    length = values.shape[3]
    angle, alternate, modes = half_angles(length)
    cosine = jnp.cos(angle)
    packed_sine = jnp.where(modes[None, :] == 0, -alternate[:, None], jnp.sin(angle))
    return jnp.stack(
        [transform_dim(values, 3, cosine), -transform_dim(values, 3, packed_sine)], axis=1
    )


def backward_packed(spectra):
    length = 2 * spectra.shape[4]
    angle, alternate, modes = half_angles(length)
    weight = jnp.where(modes == 0, 1.0, 2.0).astype(jnp.float32)
    cos_back = weight[:, None] * jnp.cos(angle.T)
    sin_back = jnp.where(modes[:, None] == 0, -alternate[None, :], 2.0 * jnp.sin(angle.T))
    return (
        transform_dim(spectra[:, 0], 3, cos_back) - transform_dim(spectra[:, 1], 3, sin_back)
    ) / length


def wave_numbers(index, length):
    signed = jnp.where(index < (length + 1) // 2, index, index - length)
    waves = signed.astype(jnp.float32) * (2.0 * jnp.pi / length)
    return jnp.where(index == length // 2, 0.0, waves)


def project(spectra, rows_x, total_x, rows_y, total_y, rows_z, total_z):
    wave_x = wave_numbers(rows_x, total_x)[:, None, None]
    wave_y = wave_numbers(rows_y, total_y)[None, :, None]
    wave_z = wave_numbers(rows_z, total_z)[None, None, :]
    wavenumber_squared = wave_x * wave_x + wave_y * wave_y + wave_z * wave_z
    denom = jnp.where(wavenumber_squared > 0, wavenumber_squared, 1.0)
    vel_real = spectra[:3, 0]
    vel_imag = spectra[:3, 1]
    source_real = spectra[3, 0]
    source_imag = spectra[3, 1]
    inner_product_real = wave_x * vel_real[0] + wave_y * vel_real[1] + wave_z * vel_real[2]
    imaginary_inner_sum = wave_x * vel_imag[0] + wave_y * vel_imag[1] + wave_z * vel_imag[2]
    waves = (wave_x, wave_y, wave_z)
    outputs = []
    for axis in range(3):
        out_real = (
            vel_real[axis]
            - waves[axis] * inner_product_real / denom
            + waves[axis] * source_imag / denom
        )
        out_imag = (
            vel_imag[axis]
            - waves[axis] * imaginary_inner_sum / denom
            - waves[axis] * source_real / denom
        )
        outputs.append(jnp.stack([out_real, out_imag], axis=0))
    return jnp.stack(outputs, axis=0)


def stream_lines(spectra):
    return forward(spectra, 2)


def span_lines(spectra):
    return forward(spectra, 3)


def stream_inverse(spectra):
    return backward(spectra, 2)


def shards(
    species,
    flow_fields,
    classes,
    diffusivity,
    left_form,
    right_form,
    stoich,
    heat_release,
    arrhenius_prefactor,
    arrhenius_energy,
    newton_matrix,
):
    params = (left_form, right_form, stoich, heat_release, arrhenius_prefactor, arrhenius_energy)
    nspec = species.shape[0]
    cells_x, cells_y, depth = (species.shape[1], species.shape[2], species.shape[3])
    total_x = cells_x * lax.axis_size("gx")
    total_y = cells_y * lax.axis_size("gy")
    fields = jnp.concatenate([species, flow_fields], axis=0)
    padded = extended(fields, (("gx", 1), ("gy", 2)), 1)
    ahead_x = padded[:, 2:, 1:-1]
    behind_x = padded[:, :-2, 1:-1]
    ahead_y = padded[:, 1:-1, 2:]
    behind_y = padded[:, 1:-1, :-2]
    ahead_z = jnp.roll(fields, -1, 3)
    behind_z = jnp.roll(fields, 1, 3)
    stream_vel = flow_fields[1][None]
    span_vel = flow_fields[2][None]
    depth_vel = flow_fields[3][None]
    laplace_sum = ahead_x + behind_x + ahead_y + behind_y + ahead_z + behind_z - 6.0 * fields
    advection = 0.5 * (
        stream_vel * (ahead_x - behind_x)
        + span_vel * (ahead_y - behind_y)
        + depth_vel * (ahead_z - behind_z)
    )
    transported = fields + TIME_STEP * (diffusivity[:, None, None, None] * laplace_sum - advection)
    columns = cells_x * cells_y
    burning_mixture_status = jnp.concatenate(
        [transported[:nspec], transported[nspec + 4 : nspec + 5]], axis=0
    ).reshape(nspec + 1, columns, depth)
    class_flat = classes.reshape(columns)
    class_value = class_flat.astype(jnp.float32)
    burning_mixture_status = substep(
        burning_mixture_status, (TIME_STEP / class_value)[:, None], newton_matrix, params
    )
    stiff = class_flat > 1
    ranking = jnp.argsort(jnp.where(stiff, 0, 1).astype(jnp.int32), stable=True)
    stiff_count = jnp.sum(stiff.astype(jnp.int32))
    stiff_cap = columns // 2
    own_slots = ranking[:stiff_cap]
    live_slots = jnp.arange(stiff_cap) < stiff_count
    buffer = burning_mixture_status[:, own_slots]
    holding_category = jnp.where(live_slots, class_value[own_slots], 1.0)
    buffer = extras(buffer, holding_category, newton_matrix, params)
    burning_mixture_status = burning_mixture_status.at[:, own_slots].set(
        jnp.where(live_slots[None, :, None], buffer, burning_mixture_status[:, own_slots])
    )
    reacted = burning_mixture_status.reshape(nspec + 1, cells_x, cells_y, depth)
    source = (reacted[nspec] - transported[nspec + 4]) / TIME_STEP
    inputs = jnp.concatenate([transported[nspec + 1 : nspec + 4], source[None]], axis=0)
    spectra = forward_packed(inputs)
    spectra = stream_lines(lax.all_to_all(spectra, "gx", split_axis=4, concat_axis=2, tiled=True))
    spectra = span_lines(lax.all_to_all(spectra, "gy", split_axis=2, concat_axis=3, tiled=True))
    local_x = spectra.shape[2]
    local_z = spectra.shape[4]
    rows_x = lax.axis_index("gy") * local_x + jnp.arange(local_x, dtype=jnp.int32)
    rows_y = jnp.arange(total_y, dtype=jnp.int32)
    rows_z = lax.axis_index("gx") * local_z + jnp.arange(local_z, dtype=jnp.int32)
    projected = project(spectra, rows_x, total_x, rows_y, total_y, rows_z, depth)
    projected = backward(projected, 3)
    projected = stream_inverse(
        lax.all_to_all(projected, "gy", split_axis=3, concat_axis=2, tiled=True)
    )
    velocity = backward_packed(
        lax.all_to_all(projected, "gx", split_axis=2, concat_axis=4, tiled=True)
    )
    species_out = reacted[:nspec]
    flow_out = jnp.concatenate(
        [transported[nspec : nspec + 1], velocity, reacted[nspec : nspec + 1]], axis=0
    )
    return (species_out, flow_out)


F32 = jnp.float32
BF16 = jnp.bfloat16
SLOT = 16
GROUP = 24
PIECE = 80
WAVES = 3 * GROUP
ROWS = WAVES + SLOT
TILE = 8
LIVE = 6
FUSED_VMEM = 40 * 2**20
FINAL_VMEM = 16 * 2**20
MESH = pl.DeviceIdType.MESH


def split_constant(array):
    high = array.astype(ml_dtypes.bfloat16)
    low = (array - high.astype(np.float64)).astype(ml_dtypes.bfloat16)
    return high, low


def spectral_constants(grid_x, grid_y, cells_x, cells_y, depth):
    devices = grid_x * grid_y
    total_x, total_y = grid_x * cells_x, grid_y * cells_y
    z = np.arange(depth)
    m = np.arange(2 * devices)
    angle = 2 * np.pi * ((m[:, None] * z[None, :]) % depth) / depth
    alternate = np.where(z % 2 == 0, 1.0, -1.0)
    into = np.stack([np.cos(angle), -np.sin(angle)], 1)
    into[0, 1] = alternate
    back = np.stack([2 * np.cos(angle), -2 * np.sin(angle)], 1)
    back[0, 0] = 1.0
    back[0, 1] = alternate
    back = (back / (depth * total_x * total_y)).reshape(devices, 2, 2, depth)
    into = into.reshape(devices, 2, 2, depth)
    kz = (m * (2 * np.pi / depth)).reshape(devices, 2, 1)
    early = np.zeros((devices, TILE, 3, depth))
    late = np.zeros((devices, TILE, 2, depth))
    out = np.zeros((devices, TILE, 3, depth))
    early[:, 0:4, 0] = into.reshape(devices, 4, depth)
    out[:, 0:4, 0] = back.reshape(devices, 4, depth)
    for mode in (0, 1):
        early[:, 4:6, 1 + mode] = kz[:, mode, :, None] * into[:, mode]
        late[:, 4, mode] = -into[:, mode, 1] / TIME_STEP
        late[:, 5, mode] = into[:, mode, 0] / TIME_STEP
        out[:, 4:6, 1 + mode] = kz[:, mode, :, None] * back[:, mode]
    early, late, out = (a.reshape(devices * TILE, -1) for a in (early, late, out))

    gx, gy = np.arange(grid_x), np.arange(grid_y)
    xl, yl = np.arange(cells_x), np.arange(cells_y)
    wave = lambda a, b, n: np.exp(-2j * np.pi * ((a[:, None] * b[None, :]) % n) / n)
    left = np.kron(wave(gx, gx, grid_x), wave(gy, gy, grid_y))
    real = np.stack([np.stack([left.real, -left.imag], -1), np.stack([left.imag, left.real], -1)], -2)
    left = np.einsum("kgrs,pq->kprgqs", real, np.eye(TILE // 2)).reshape(TILE * devices, -1)
    twist = np.kron(wave(gx, xl, total_x), wave(gy, yl, total_y))
    twist = np.tile(twist, (1, 2))
    inner = np.kron(wave(xl, xl, cells_x), wave(yl, yl, cells_y))
    pair = np.eye(2)
    right = np.concatenate([np.kron(pair, inner.real), np.kron(pair, inner.imag)], 0)
    unright = np.concatenate([np.kron(pair, inner.real), -np.kron(pair, inner.imag)], 0)

    def waves(index, length):
        signed = np.where(index < (length + 1) // 2, index, index - length) * (2 * np.pi / length)
        return np.where(index == length // 2, 0.0, signed)

    kx = waves(gx[:, None] + grid_x * xl[None, :], total_x)
    ky = waves(gy[:, None] + grid_y * yl[None, :], total_y)
    shape = (grid_x, grid_y, cells_x, cells_y)
    kx = np.broadcast_to(kx[:, None, :, None], shape).reshape(devices, cells_x * cells_y)
    ky = np.broadcast_to(ky[None, :, None, :], shape).reshape(devices, cells_x * cells_y)
    kxy = np.concatenate([kx, ky], -1)
    square = np.concatenate([kx * kx + ky * ky] * 2, -1)
    matrices = []
    for matrix in (early, late, left, right, unright, left.T):
        matrices.extend(split_constant(matrix))
    matrices = np.ascontiguousarray(np.concatenate(matrices, 1))
    tables = np.ascontiguousarray(np.stack([twist.real, twist.imag, kxy, square]), dtype=np.float32)[:, :, None, :]
    return matrices, tables, *(np.ascontiguousarray(a) for a in split_constant(out))


def halves(value):
    high = value.astype(BF16)
    low = (value - high.astype(F32)).astype(BF16)
    return high, low


def mul(a, b):
    return jnp.dot(a, b, preferred_element_type=F32)


def mul_t(a, b):
    return lax.dot_general(a, b, (((1,), (1,)), ((), ())), preferred_element_type=F32)


def precise(a, b):
    return jnp.dot(a, b, precision=PRECISE, preferred_element_type=F32)


def turn(value):
    rows = value.shape[1]
    parity = lax.broadcasted_iota(jnp.int32, value.shape, 1) % 2
    return jnp.where(parity == 0, -pltpu.roll(value, rows - 1, 1), pltpu.roll(value, 1, 1))


def flame_kernel(
    grid_x, grid_y, species_hbm, flow_hbm, kinds_hbm, diffusivity_hbm, left_hbm, right_hbm, stoich_hbm, heat_hbm,
    prefactor_hbm, energy_hbm, newton_hbm, matrices_hbm, tables_hbm,
    species_out, flow_out, gathered_out,
    fields, moved, speed, halo_x, halo_y, edges, state, angles, trial, stacked, span,
    kinds, diffusivity, left_in, right_in, stoich_in, heat_in, prefactor_in, energy_in, newton_in,
    forms_t, newton_pad, weights_f, matrices, tables, inverse, packed, spectra, unpacked, gathered,
    load_sem, small_sem, big_sem, halo_send, halo_recv, out_send, out_recv, back_send, back_recv,
):
    devices = grid_x * grid_y
    gx, gy = lax.axis_index("gx"), lax.axis_index("gy")
    me = gx * grid_y + gy
    nspec = species_hbm.shape[0]
    nfield, columns, depth = fields.shape
    nflow = nfield - nspec
    cells_x, cells_y = kinds.shape
    nreac = heat_in.shape[1]

    def peer(offset):
        other = lax.rem(me + offset, devices)
        return other, {"gx": other // grid_y, "gy": lax.rem(other, grid_y)}

    barrier = pltpu.get_barrier_semaphore()
    loads = (
        pltpu.make_async_copy(species_hbm, fields.at[pl.ds(0, nspec)], load_sem.at[0]),
        pltpu.make_async_copy(flow_hbm, fields.at[pl.ds(nspec, nflow)], load_sem.at[1]),
    )
    for load in loads:
        load.start()
    smalls = []
    for source, target in (
        (diffusivity_hbm, diffusivity), (kinds_hbm, kinds), (left_hbm, left_in), (right_hbm, right_in),
        (stoich_hbm, stoich_in), (heat_hbm, heat_in), (prefactor_hbm, prefactor_in), (energy_hbm, energy_in),
        (newton_hbm, newton_in),
    ):
        smalls.append(pltpu.make_async_copy(source, target, small_sem.at[len(smalls)]))
        smalls[-1].start()
    bigs = (
        pltpu.make_async_copy(matrices_hbm, matrices, big_sem.at[0]),
        pltpu.make_async_copy(tables_hbm, tables, big_sem.at[1]),
    )

    @pl.loop(1, devices)
    def greet(offset):
        pl.semaphore_signal(barrier, inc=1, device_id=peer(offset)[1], device_id_type=MESH)

    state[...] = jnp.zeros_like(state)
    spectra[:, LIVE:TILE, :] = jnp.zeros((devices, TILE - LIVE, depth), F32)
    gathered[:, LIVE:TILE, :] = jnp.zeros((devices, TILE - LIVE, depth), F32)
    forms_t[...] = jnp.zeros_like(forms_t)
    newton_pad[...] = jnp.zeros_like(newton_pad)
    weights_f[...] = jnp.zeros_like(weights_f)
    for load in loads:
        load.wait()
    for big in bigs:
        big.start()
    for f in range(nfield):
        edges[0, f] = fields[f, pl.ds(0, cells_x, stride=cells_y), :]
        edges[1, f] = fields[f, pl.ds(cells_y - 1, cells_x, stride=cells_y), :]

    up_x = {"gx": lax.rem(gx + 1, grid_x), "gy": gy}
    down_x = {"gx": lax.rem(gx + grid_x - 1, grid_x), "gy": gy}
    up_y = {"gx": gx, "gy": lax.rem(gy + 1, grid_y)}
    down_y = {"gx": gx, "gy": lax.rem(gy + grid_y - 1, grid_y)}
    swaps = []
    for at, (source, target, device) in enumerate((
        (edges.at[1], halo_y.at[0], up_y),
        (edges.at[0], halo_y.at[1], down_y),
        (fields.at[:, pl.ds(columns - cells_y, cells_y)], halo_x.at[0], up_x),
        (fields.at[:, pl.ds(0, cells_y)], halo_x.at[1], down_x),
    )):
        swaps.append(pltpu.make_async_remote_copy(
            src_ref=source, dst_ref=target, send_sem=halo_send.at[at], recv_sem=halo_recv.at[at],
            device_id=device, device_id_type=MESH))

    def swap():
        pl.semaphore_wait(barrier, devices - 1)
        for copy in swaps:
            copy.start()

    reach = gx // 2 + gy // 2 + lax.rem(gy, 2)
    pl.when(reach >= 4)(swap)

    for small in smalls:
        small.wait()
    forms_t[0:nspec, 0:nreac] = left_in[...]
    forms_t[0:nspec, GROUP : GROUP + nreac] = right_in[...]
    forms_t[nspec : nspec + 1, 2 * GROUP : 2 * GROUP + nreac] = 0.5 * energy_in[...]
    base = forms_t[0:SLOT, :]
    high = base.astype(BF16).astype(F32)
    low = (base - high).astype(BF16).astype(F32)
    row = lax.broadcasted_iota(jnp.int32, (SLOT, depth), 0)
    lane = lax.broadcasted_iota(jnp.int32, (SLOT, depth), 1)
    forms_t[3 * SLOT : 4 * SLOT, :] = base + jnp.where(lane == row + WAVES, 1.0, 0.0)
    forms_t[0:SLOT, :] = high
    forms_t[SLOT : 2 * SLOT, :] = high
    forms_t[2 * SLOT : 3 * SLOT, :] = low
    turned_forms = jnp.transpose(forms_t[...])
    forms = turned_forms[:WAVES, : 3 * SLOT].astype(BF16)
    lift = turned_forms[:ROWS, 3 * SLOT : 4 * SLOT]
    forms_t[...] = jnp.zeros_like(forms_t)
    forms_t[0:nspec, 0:nreac] = stoich_in[...] * (0.5 * prefactor_in[...])
    forms_t[nspec : nspec + 1, 0:nreac] = heat_in[...] * (0.5 * prefactor_in[...])
    newton_pad[0 : nspec + 1, 0 : nspec + 1] = newton_in[...]
    newton = newton_pad[:, 0:SLOT]
    gain0 = precise(newton, forms_t[0:SLOT, :])
    gain1 = gain0 - precise(newton, gain0)
    gain2 = gain1 - precise(newton, gain1)
    gains = gain2 + pltpu.roll(gain1, GROUP, 1) + pltpu.roll(gain0, 2 * GROUP, 1)
    mixed = precise(lift, gains)
    high = mixed.astype(BF16).astype(F32)
    low = mixed - high
    for at in range(3):
        part = slice(at * GROUP, (at + 1) * GROUP)
        for place, value in enumerate((high, high, low)):
            begin = at * PIECE + place * GROUP
            weights_f[:, begin : begin + GROUP] = value[:, part]
    weights = weights_f[:, : 3 * PIECE].astype(BF16)
    last, middle = weights[:WAVES, 2 * PIECE :], weights[:WAVES, PIECE:]

    for axis in range(3):
        speed[axis] = fields[nspec + 1 + axis] * (0.5 * TIME_STEP)
    rows = lax.broadcasted_iota(jnp.int32, (cells_y, depth), 0)

    @pl.loop(0, nfield)
    def transport(f):
        coefficient = diffusivity[f] * TIME_STEP
        centre = 1.0 - 6.0 * coefficient
        for x in range(cells_x):
            at = pl.ds(x * cells_y, cells_y)
            here = fields[f, at]
            ahead_y = jnp.where(rows == cells_y - 1, 0.0, pltpu.roll(here, cells_y - 1, 0))
            behind_y = jnp.where(rows == 0, 0.0, pltpu.roll(here, 1, 0))
            ahead_z = pltpu.roll(here, depth - 1, 1)
            behind_z = pltpu.roll(here, 1, 1)
            total = ahead_y + behind_y + ahead_z + behind_z
            drift = speed[1, at] * (ahead_y - behind_y) + speed[2, at] * (ahead_z - behind_z)
            if 0 < x < cells_x - 1:
                ahead_x, behind_x = fields[f, pl.ds((x + 1) * cells_y, cells_y)], fields[f, pl.ds((x - 1) * cells_y, cells_y)]
                total = total + (ahead_x + behind_x)
                drift = drift + speed[0, at] * (ahead_x - behind_x)
            elif x == 0:
                ahead_x = fields[f, pl.ds(cells_y, cells_y)]
                total = total + ahead_x
                drift = drift + speed[0, at] * ahead_x
            else:
                behind_x = fields[f, pl.ds((x - 1) * cells_y, cells_y)]
                total = total + behind_x
                drift = drift - speed[0, at] * behind_x
            moved[f, at] = here * centre + (coefficient * total - drift)

    def source_of(f):
        return f if f < nspec else nfield - 1

    for f in range(nspec + 1):
        for x in range(1, cells_x - 1):
            state[pl.ds(x * cells_y * SLOT + f, cells_y, stride=SLOT), :] = moved[source_of(f), pl.ds(x * cells_y, cells_y)]

    def tile(column):
        return pl.ds(column * SLOT, SLOT)

    def rates(wave, step):
        curve = jnp.tanh(wave)
        rate = (1.0 + curve[2 * GROUP :]) * curve[:GROUP] * curve[GROUP : 2 * GROUP] * step
        high = rate.astype(BF16).astype(F32)
        low = rate - high
        pad = jnp.zeros((PIECE - 3 * GROUP, rate.shape[1]), F32)
        return jnp.concatenate([high, low, high, pad], axis=0).astype(BF16)

    def react(members):
        pairs = [members[i : i + 2] for i in range(0, len(members), 2)]
        wide = 2 * depth
        for at, pair in enumerate(pairs):
            value = jnp.concatenate([state[tile(c), :] for c in pair], axis=1)
            high, low = halves(value)
            angles[at] = mul(forms, jnp.concatenate([high, low, high], axis=0))
            for half, c in enumerate(pair):
                kind = jnp.full((TILE, depth), kinds[c // cells_y, c % cells_y], jnp.int32)
                span[at, :, half * depth : (half + 1) * depth] = kind.astype(F32)

        @pl.loop(0, 4)
        def section(number):
            limit = number.astype(F32)
            for at, pair in enumerate(pairs):
                spans = span[at]
                step = jnp.where(spans > limit, TIME_STEP / spans, 0.0)
                trial[at, WAVES:ROWS, :] = jnp.concatenate([step, step], axis=0)
                wave = angles[at]
                piece = rates(wave, jnp.concatenate([step] * 3, axis=0))
                stacked[at, 0:PIECE, :] = piece
                trial[at, 0:WAVES, :] = wave + mul(last, piece)
            for at, pair in enumerate(pairs):
                step = trial[at, WAVES : WAVES + TILE, :]
                stacked[at, PIECE : 2 * PIECE, :] = rates(trial[at, 0:WAVES, :], jnp.concatenate([step] * 3, axis=0))
                trial[at, 0:WAVES, :] = angles[at] + mul(middle, stacked[at, 0 : 2 * PIECE, :])
            for at, pair in enumerate(pairs):
                step = trial[at, WAVES : WAVES + TILE, :]
                stacked[at, 2 * PIECE : 3 * PIECE, :] = rates(trial[at, 0:WAVES, :], jnp.concatenate([step] * 3, axis=0))
                change = mul(weights, stacked[at])
                angles[at] = angles[at] + change[:WAVES]
                for half, c in enumerate(pair):
                    state[tile(c), :] = state[tile(c), :] + change[WAVES:, half * depth : (half + 1) * depth]

    pl.when(reach == 3)(swap)
    react([x * cells_y + y for x in range(1, cells_x - 1) for y in range(1, cells_y - 1)])
    pl.when(reach <= 2)(swap)

    for big in bigs:
        big.wait()
    lane = lax.broadcasted_iota(jnp.int32, (1, TILE, depth), 2)
    row = lax.broadcasted_iota(jnp.int32, (1, TILE, depth), 1)
    kz = (2 * me + row // 2).astype(F32) * (2.0 * np.pi / depth)
    square = tables[3] + kz * kz
    inverse[...] = 1.0 / jnp.where(square > 0, square, 1.0)

    for copy in swaps[2:]:
        copy.wait()
    for copy in swaps[:2]:
        copy.wait()
    first, final = pl.ds(0, cells_y), pl.ds(columns - cells_y, cells_y)
    low_y, high_y = pl.ds(0, cells_x, stride=cells_y), pl.ds(cells_y - 1, cells_x, stride=cells_y)
    for f in range(nfield):
        coefficient = diffusivity[f] * TIME_STEP
        moved[f, first] = moved[f, first] + halo_x[0, f] * (coefficient + speed[0, first])
        moved[f, final] = moved[f, final] + halo_x[1, f] * (coefficient - speed[0, final])
        moved[f, low_y, :] = moved[f, low_y, :] + halo_y[0, f] * (coefficient + speed[1, low_y, :])
        moved[f, high_y, :] = moved[f, high_y, :] + halo_y[1, f] * (coefficient - speed[1, high_y, :])
    for f in range(nspec + 1):
        source = source_of(f)
        for x in (0, cells_x - 1):
            state[pl.ds(x * cells_y * SLOT + f, cells_y, stride=SLOT), :] = moved[source, pl.ds(x * cells_y, cells_y)]
        for y in (0, cells_y - 1):
            state[pl.ds(y * SLOT + f, cells_x, stride=cells_y * SLOT), :] = moved[source, pl.ds(y, cells_x, stride=cells_y), :]

    sizes = [3 * depth, 3 * depth, 2 * depth, 2 * depth] + [2 * depth] * 2 + [depth] * 4 + [2 * depth] * 2
    starts = [sum(sizes[:i]) for i in range(len(sizes))]

    def matrix(at):
        return matrices[:, starts[at] : starts[at] + sizes[at]]

    def dot_left(at, value, product=mul):
        high, low = halves(value)
        a, b = matrix(at), matrix(at + 1)
        return product(a, high) + product(a, low) + product(b, high)

    def dot_right(value, at):
        high, low = halves(value)
        a, b = matrix(at), matrix(at + 1)
        return mul(high, a) + mul(low, a) + mul(high, b)

    none = jnp.zeros((columns, depth), F32)
    u, v, w = (moved[nspec + 1 + axis] for axis in range(3))
    lines = jnp.concatenate([jnp.concatenate([u, w, none], axis=1), jnp.concatenate([v, none, w], axis=1)], axis=0)
    packed[...] = dot_left(0, lines, mul_t).reshape(packed.shape)

    react([x * cells_y + y for x in (0, cells_x - 1) for y in range(1, cells_y - 1)]
          + [x * cells_y + y for y in (0, cells_y - 1) for x in range(cells_x)])

    for x in range(cells_x):
        hot = state[pl.ds(x * cells_y * SLOT + nspec, cells_y, stride=SLOT), :]
        flow_out[nflow - 1, pl.ds(x * cells_y, cells_y)] = hot
    warmth = flow_out[nflow - 1] - moved[nfield - 1]
    lines = jnp.concatenate([jnp.concatenate([warmth, none], axis=1), jnp.concatenate([none, warmth], axis=1)], axis=0)
    packed[...] = packed[...] + dot_left(2, lines, mul_t).reshape(packed.shape)

    live = pl.ds(0, LIVE)

    def exchange(source, target, send_sem, recv_sem, meanwhile):
        @pl.loop(1, devices)
        def start(offset):
            other, device = peer(offset)
            pltpu.make_async_remote_copy(
                src_ref=source.at[other, live], dst_ref=target.at[me, live],
                send_sem=send_sem.at[other], recv_sem=recv_sem.at[me],
                device_id=device, device_id_type=MESH).start()

        target[me, live] = source[me, live]
        meanwhile()

        @pl.loop(1, devices)
        def finish(offset):
            other, device = peer(offset)
            pltpu.make_async_remote_copy(
                src_ref=source.at[other, live], dst_ref=target.at[other, live],
                send_sem=send_sem.at[other], recv_sem=recv_sem.at[other],
                device_id=device, device_id_type=MESH).wait()

    def outputs():
        for f in range(nspec):
            for x in range(cells_x):
                species_out[f, pl.ds(x * cells_y, cells_y)] = state[pl.ds(x * cells_y * SLOT + f, cells_y, stride=SLOT), :]
        for f in range(nflow - 1):
            flow_out[f] = moved[nspec + f]

    exchange(packed, spectra, out_send, out_recv, outputs)

    shape = spectra.shape
    flat = (shape[0] * shape[1], shape[2])
    value = dot_left(4, spectra[...].reshape(flat)).reshape(shape)
    turned = turn(value)
    re, im = tables[0], tables[1]
    a = value * re + turned * im
    b = turned * re - value * im
    value = dot_right(jnp.concatenate([a.reshape(flat), b.reshape(flat)], axis=1), 6).reshape(shape)

    kxy = tables[2]
    upper = lane < columns
    total = kxy * value
    total = total + pltpu.roll(total, columns, 2)
    crossed = pltpu.roll(value, columns, 2)
    even = pltpu.roll(jnp.where(upper, value, crossed), 4, 1)
    odd = pltpu.roll(jnp.where(upper, crossed, value), 6, 1)
    potential = (total + jnp.where(row < 2, even, odd)) * inverse[...]
    deep = jnp.where(upper, pltpu.roll(potential, 4, 1), pltpu.roll(potential, 2, 1))
    value = jnp.where(row < 4, kxy * potential, jnp.where(row < LIVE, deep, 0.0))

    turned = turn(value)
    value = dot_right(jnp.concatenate([value.reshape(flat), turned.reshape(flat)], axis=1), 8).reshape(shape)
    value = value * re - turn(value) * im
    unpacked[...] = dot_left(10, value.reshape(flat)).reshape(shape)
    exchange(unpacked, gathered, back_send, back_recv, lambda: None)
    gathered_out[...] = gathered[...]


def final_kernel(back_h, back_l, species_in, flow_in, gathered, species_hbm, flow_hbm, flow, sems):
    nflow, columns, depth = flow.shape
    store = pltpu.make_async_copy(species_in, species_hbm, sems.at[0])
    store.start()
    value = jnp.transpose(gathered[...].reshape(back_h.shape[0], 2 * columns))
    high, low = halves(value)
    a, b = back_h[...], back_l[...]
    result = mul(high, a) + mul(low, a) + mul(high, b)
    flow[0] = flow_in[0]
    flow[1] = flow_in[1] - result[:columns, :depth]
    flow[2] = flow_in[2] - result[columns:, :depth]
    flow[3] = flow_in[3] - (result[:columns, depth : 2 * depth] + result[columns:, 2 * depth :])
    flow[4] = flow_in[4]
    ship = pltpu.make_async_copy(flow, flow_hbm, sems.at[1])
    ship.start()
    store.wait()
    ship.wait()


def flame(
    species, flow_fields, classes, diffusivity, left_form, right_form, stoich, heat_release,
    arrhenius_prefactor, arrhenius_energy, newton_matrix, matrices, tables, back_h, back_l,
):
    grid_x, grid_y = lax.axis_size("gx"), lax.axis_size("gy")
    nspec, cells_x, cells_y, depth = species.shape
    nflow = flow_fields.shape[0]
    nfield = nspec + nflow
    nreac = left_form.shape[0]
    columns = cells_x * cells_y
    devices = grid_x * grid_y
    hbm = pl.BlockSpec(memory_space=pltpu.HBM)
    vmem = pl.BlockSpec(memory_space=pltpu.VMEM)
    dma = pltpu.SemaphoreType.DMA
    box = (devices, TILE, depth)
    shaped = lambda shape: jax.ShapeDtypeStruct(shape, F32)
    line = lambda a: a.reshape(1, -1)
    inputs = (
        species.reshape(nspec, columns, depth), flow_fields.reshape(nflow, columns, depth), classes, diffusivity,
        left_form.T, right_form.T, stoich.T, line(heat_release), line(arrhenius_prefactor), line(arrhenius_energy),
        newton_matrix, matrices, tables,
    )
    most = (max((cells_x - 2) * (cells_y - 2), columns) + 1) // 2
    scratch = [
        pltpu.VMEM((nfield, columns, depth), F32),
        pltpu.VMEM((nfield, columns, depth), F32),
        pltpu.VMEM((3, columns, depth), F32),
        pltpu.VMEM((2, nfield, cells_y, depth), F32),
        pltpu.VMEM((2, nfield, cells_x, depth), F32),
        pltpu.VMEM((2, nfield, cells_x, depth), F32),
        pltpu.VMEM((columns * SLOT, depth), F32),
        pltpu.VMEM((most, WAVES, 2 * depth), F32),
        pltpu.VMEM((most, ROWS, 2 * depth), F32),
        pltpu.VMEM((most, 3 * PIECE, 2 * depth), BF16),
        pltpu.VMEM((most, TILE, 2 * depth), F32),
        pltpu.SMEM(classes.shape, jnp.int32),
        pltpu.SMEM(diffusivity.shape, F32),
    ]
    scratch += [pltpu.VMEM(a.shape, F32) for a in inputs[4:11]]
    scratch += [
        pltpu.VMEM((depth, depth), F32),
        pltpu.VMEM((SLOT, depth), F32),
        pltpu.VMEM((ROWS, 2 * depth), F32),
        pltpu.VMEM(matrices.shape, BF16),
        pltpu.VMEM(tables.shape, F32),
    ]
    scratch += [pltpu.VMEM(box, F32)] * 5
    scratch += [dma((2,)), dma((9,)), dma((2,)), dma((4,)), dma((4,))] + [dma((devices,))] * 4
    species_done, flow_done, gathered = pl.pallas_call(
        functools.partial(flame_kernel, grid_x, grid_y),
        out_shape=(shaped((nspec, columns, depth)), shaped((nflow, columns, depth)), shaped(box)),
        in_specs=[hbm] * len(inputs),
        out_specs=(vmem, vmem, vmem),
        scratch_shapes=scratch,
        compiler_params=pltpu.CompilerParams(collective_id=0, has_side_effects=True, vmem_limit_bytes=FUSED_VMEM),
        name="flame",
    )(*inputs)
    species_out, flow_out = pl.pallas_call(
        final_kernel,
        out_shape=(shaped((nspec, columns, depth)), shaped((nflow, columns, depth))),
        in_specs=[vmem] * 5,
        out_specs=(hbm, hbm),
        scratch_shapes=[pltpu.VMEM((nflow, columns, depth), F32), dma((2,))],
        compiler_params=pltpu.CompilerParams(vmem_limit_bytes=FINAL_VMEM),
        name="final",
    )(back_h, back_l, species_done, flow_done, gathered)
    return species_out.reshape(species.shape), flow_out.reshape(flow_fields.shape)


def solution(mesh):
    grid_x, grid_y = mesh.shape["gx"], mesh.shape["gy"]

    def step(species, flow_fields, classes, *rest):
        cells_x = species.shape[1] // grid_x
        cells_y = species.shape[2] // grid_y
        depth = species.shape[3]
        direct = (
            depth == 128 and cells_y == 8 and 2 * cells_x * cells_y == 128
            and depth == 4 * grid_x * grid_y
        )
        grids = (P(None, "gx", "gy", None), P(None, "gx", "gy", None), P("gx", "gy"))
        constants = ()
        if direct:
            constants = tuple(spectral_constants(grid_x, grid_y, cells_x, cells_y, depth))
        return jax.shard_map(
            flame if direct else shards,
            mesh=mesh,
            in_specs=grids + (P(),) * (len(rest) + len(constants)),
            out_specs=(P(None, "gx", "gy", None), P(None, "gx", "gy", None)),
            check_vma=False,
        )(species, flow_fields, classes, *rest, *constants)

    return step
```

time: 44.5 us -> 43.9 us (0.987); the launches traced: 45.4 us -> 43.4 us
  Pallas kernels: 41 us -> 32.6 us
  local copies, waits for them, and re-layouts: 3.35 us -> 10.2 us
    pallas_call x3 -> x2, Pallas kernels: 41 us -> 32.6 us  [the longest x1 31.6 us: flame(): pl.pallas_call(functools.partial(flame_kernel, grid_x, grid_y), out_shape...]
    unnamed x55 -> x30, local copies, waits for them, and re-layouts: 3.35 us -> 10.2 us
where the time goes in v1:
time: 43.9 us; the launch traced here: 43.4 us
  Pallas kernels  32.6 us (74%)
  local copies, waits for them, and re-layouts  10.2 us (23%)
  between operations  0.68 us (2%)
    pallas_call x1, Pallas kernels, flame(): pl.pallas_call(functools.partial(flame_kernel, grid_x, grid_y), out_shape...  31.6 us
    unnamed x30, local copies, waits for them, and re-layouts  10.2 us
    pallas_call x1, Pallas kernels, flame(): pl.pallas_call(final_kernel, out_shape=(shaped((nspec, columns, depth)),...  1.01 us

profile of v1, /device:TPU:0, one launch (start us, length us, event | category | flops | bytes accessed | tf_op | source)
XLA Modules:
  0.0 43.4 jit_solution(3600995634572310770)
XLA Ops:
  0.6 0.0 copy-start
  0.6 1.4 %copy-done = bf16[256,2816]{1,0:T(8,128)(2,1)S(1)} copy-done((bf16[256,2816]{1,0:T(8,128)(2,1)S(1)}, bf16[256,2816]{1,0:T(8,128)(2,1)}, u32[]{:S(2)}) %copy-start) | copy-done | bytes 1441816
  2.0 0.0 copy-start.1
  2.0 1.0 %copy-done.1 = f32[9,8,8,128]{3,2,1,0:T(8,128)S(1)} copy-done((f32[9,8,8,128]{3,2,1,0:T(8,128)S(1)}, f32[9,8,8,128]{3,2,1,0:T(8,128)}, u32[]{:S(2)}) %copy-start.1) | copy-done | bytes 294936
  3.0 0.0 copy-start.4
  3.0 0.9 %copy-done.4 = f32[5,8,8,128]{3,2,1,0:T(8,128)S(1)} copy-done((f32[5,8,8,128]{3,2,1,0:T(8,128)S(1)}, f32[5,8,8,128]{3,2,1,0:T(8,128)}, u32[]{:S(2)}) %copy-start.4) | copy-done | bytes 163864
  3.9 0.0 copy-start.5
  3.9 0.8 %copy-done.5 = f32[4,32,1,128]{3,2,1,0:T(1,128)S(1)} copy-done((f32[4,32,1,128]{3,2,1,0:T(1,128)S(1)}, f32[4,32,1,128]{3,2,1,0:T(1,128)}, u32[]{:S(2)}) %copy-start.5) | copy-done | bytes 65560
  4.7 0.0 copy-start.6
  4.7 0.7 %copy-done.6 = f32[19,9]{0,1:T(8,128)S(1)} copy-done((f32[19,9]{0,1:T(8,128)S(1)}, f32[19,9]{0,1:T(8,128)}, u32[]{:S(2)}) %copy-start.6) | copy-done | bytes 708
  5.4 0.0 copy-start.7
  5.4 0.7 %copy-done.7 = f32[19,9]{0,1:T(8,128)S(1)} copy-done((f32[19,9]{0,1:T(8,128)S(1)}, f32[19,9]{0,1:T(8,128)}, u32[]{:S(2)}) %copy-start.7) | copy-done | bytes 708
  6.1 0.0 copy-start.8
  6.1 0.7 %copy-done.8 = f32[19,9]{0,1:T(8,128)S(1)} copy-done((f32[19,9]{0,1:T(8,128)S(1)}, f32[19,9]{0,1:T(8,128)}, u32[]{:S(2)}) %copy-start.8) | copy-done | bytes 708
  6.8 0.0 copy-start.9
  6.8 0.7 %copy-done.9 = f32[10,10]{1,0:T(8,128)S(1)} copy-done((f32[10,10]{1,0:T(8,128)S(1)}, f32[10,10]{1,0:T(8,128)}, u32[]{:S(2)}) %copy-start.9) | copy-done | bytes 424
  7.5 0.0 copy-start.10
  7.5 0.7 %copy-done.10 = s32[8,8]{1,0:T(8,128)S(1)} copy-done((s32[8,8]{1,0:T(8,128)S(1)}, s32[8,8]{1,0:T(8,128)}, u32[]{:S(2)}) %copy-start.10) | copy-done | bytes 280
  8.2 0.0 copy-start.11
  8.2 0.7 %copy-done.11 = f32[14]{0:T(128)S(1)} copy-done((f32[14]{0:T(128)S(1)}, f32[14]{0:T(128)}, u32[]{:S(2)}) %copy-start.11) | copy-done | bytes 80
  8.9 0.0 copy-start.12
  8.9 0.7 %copy-done.12 = f32[19]{0:T(128)S(1)} copy-done((f32[19]{0:T(128)S(1)}, f32[19]{0:T(128)}, u32[]{:S(2)}) %copy-start.12) | copy-done | bytes 100
  9.5 0.0 copy-start.13
  9.5 0.7 %copy-done.13 = f32[19]{0:T(128)S(1)} copy-done((f32[19]{0:T(128)S(1)}, f32[19]{0:T(128)}, u32[]{:S(2)}) %copy-start.13) | copy-done | bytes 100
  10.2 0.0 copy-start.14
  10.2 0.7 %copy-done.14 = f32[19]{0:T(128)S(1)} copy-done((f32[19]{0:T(128)S(1)}, f32[19]{0:T(128)}, u32[]{:S(2)}) %copy-start.14) | copy-done | bytes 100
  10.8 0.0 copy-start.2
  10.8 0.0 copy-start.3
  10.8 31.6 %flame.1 = (f32[9,64,128]{2,1,0:T(8,128)S(1)}, f32[5,64,128]{2,1,0:T(8,128)S(1)}, f32[32,8,128]{2,1,0:T(8,128)S(1)}) custom-call(f32[9,64,128]{2,1,0:T(8,128)S(1)} %bitcast.10, f32[5,64,128]{2,1,0:T(8,128)S(1)} %bitcast.11, s32[8,8]{1,0:T(8,128)S(1)} %copy-done.10, f32[14]{0:T(128)S(1)} %copy-done.11, f32[9,19]{1,0:T(8,128)S(1)} %bitcast.12, ...), custom_call_target="tpu_custom_call" | custom-call | tf_op jit(solution)/shard_map/flame/pallas_call | solution.py:753
  42.4 0.0 copy-done.2
  42.4 0.0 copy-done.3
  42.4 1.0 %final.1 = (f32[9,64,128]{2,1,0:T(8,128)}, f32[5,64,128]{2,1,0:T(8,128)}) custom-call(bf16[256,384]{1,0:T(8,128)(2,1)S(1)} %copy-done.3, bf16[256,384]{1,0:T(8,128)(2,1)S(1)} %copy-done.2, f32[9,64,128]{2,1,0:T(8,128)S(1)} %get-tuple-element.7.species_in, f32[5,64,128]{2,1,0:T(8,128)S(1)} %get-tuple-element.8.flow_in, ...), custom_call_target="tpu_custom_call" | custom-call | tf_op jit(solution)/shard_map/final/pallas_call | solution.py:762
Async XLA Ops:
  0.6 1.4 %copy-start = (bf16[256,2816]{1,0:T(8,128)(2,1)S(1)}, bf16[256,2816]{1,0:T(8,128)(2,1)}, u32[]{:S(2)}) copy-start(bf16[256,2816]{1,0:T(8,128)(2,1)} %constant.8.clone.matrices_hbm) | copy-start | bytes 4325380
  2.0 1.0 %copy-start.1 = (f32[9,8,8,128]{3,2,1,0:T(8,128)S(1)}, f32[9,8,8,128]{3,2,1,0:T(8,128)}, u32[]{:S(2)}) copy-start(f32[9,8,8,128]{3,2,1,0:T(8,128)} %param.15) | copy-start | bytes 884740
  3.0 0.9 %copy-start.4 = (f32[5,8,8,128]{3,2,1,0:T(8,128)S(1)}, f32[5,8,8,128]{3,2,1,0:T(8,128)}, u32[]{:S(2)}) copy-start(f32[5,8,8,128]{3,2,1,0:T(8,128)} %param.16) | copy-start | bytes 491524
  3.9 0.8 %copy-start.5 = (f32[4,32,1,128]{3,2,1,0:T(1,128)S(1)}, f32[4,32,1,128]{3,2,1,0:T(1,128)}, u32[]{:S(2)}) copy-start(f32[4,32,1,128]{3,2,1,0:T(1,128)} %constant.9.clone.tables_hbm) | copy-start | bytes 196612
  4.7 0.7 %copy-start.6 = (f32[19,9]{0,1:T(8,128)S(1)}, f32[19,9]{0,1:T(8,128)}, u32[]{:S(2)}) copy-start(f32[19,9]{0,1:T(8,128)} %param.19) | copy-start | bytes 2056
  5.4 0.7 %copy-start.7 = (f32[19,9]{0,1:T(8,128)S(1)}, f32[19,9]{0,1:T(8,128)}, u32[]{:S(2)}) copy-start(f32[19,9]{0,1:T(8,128)} %param.20) | copy-start | bytes 2056
  6.1 0.7 %copy-start.8 = (f32[19,9]{0,1:T(8,128)S(1)}, f32[19,9]{0,1:T(8,128)}, u32[]{:S(2)}) copy-start(f32[19,9]{0,1:T(8,128)} %param.21) | copy-start | bytes 2056
  6.8 0.7 %copy-start.9 = (f32[10,10]{1,0:T(8,128)S(1)}, f32[10,10]{1,0:T(8,128)}, u32[]{:S(2)}) copy-start(f32[10,10]{1,0:T(8,128)} %newton_hbm.1) | copy-start | bytes 1204
  7.5 0.7 %copy-start.10 = (s32[8,8]{1,0:T(8,128)S(1)}, s32[8,8]{1,0:T(8,128)}, u32[]{:S(2)}) copy-start(s32[8,8]{1,0:T(8,128)} %kinds_hbm.1) | copy-start | bytes 772
  8.2 0.7 %copy-start.11 = (f32[14]{0:T(128)S(1)}, f32[14]{0:T(128)}, u32[]{:S(2)}) copy-start(f32[14]{0:T(128)} %diffusivity_hbm.1) | copy-start | bytes 172
  8.9 0.7 %copy-start.12 = (f32[19]{0:T(128)S(1)}, f32[19]{0:T(128)}, u32[]{:S(2)}) copy-start(f32[19]{0:T(128)} %param.22) | copy-start | bytes 232
  9.5 0.7 %copy-start.13 = (f32[19]{0:T(128)S(1)}, f32[19]{0:T(128)}, u32[]{:S(2)}) copy-start(f32[19]{0:T(128)} %param.23) | copy-start | bytes 232
  10.2 0.7 %copy-start.14 = (f32[19]{0:T(128)S(1)}, f32[19]{0:T(128)}, u32[]{:S(2)}) copy-start(f32[19]{0:T(128)} %param.24) | copy-start | bytes 232
  10.8 31.6 %copy-start.2 = (bf16[256,384]{1,0:T(8,128)(2,1)S(1)}, bf16[256,384]{1,0:T(8,128)(2,1)}, u32[]{:S(2)}) copy-start(bf16[256,384]{1,0:T(8,128)(2,1)} %constant.11.clone.back_l) | copy-start | bytes 589828
  10.8 31.6 %copy-start.3 = (bf16[256,384]{1,0:T(8,128)(2,1)S(1)}, bf16[256,384]{1,0:T(8,128)(2,1)}, u32[]{:S(2)}) copy-start(bf16[256,384]{1,0:T(8,128)(2,1)} %constant.10.clone.back_h) | copy-start | bytes 589828

commit v2 on v1

--- a/solution.py
+++ b/solution.py
@@ -758,7 +758,7 @@
         scratch_shapes=scratch,
         compiler_params=pltpu.CompilerParams(collective_id=0, has_side_effects=True, vmem_limit_bytes=FUSED_VMEM),
         name="flame",
-    )(*inputs)
+    )(*[pltpu.with_memory_space_constraint(a, pltpu.HBM) for a in inputs])
     species_out, flow_out = pl.pallas_call(
         final_kernel,
         out_shape=(shaped((nspec, columns, depth)), shaped((nflow, columns, depth))),

time: 43.9 us -> 33.3 us (0.76)
  local copies, waits for them, and re-layouts: 10.2 us -> 0.01 us
    unnamed x30 -> x4, local copies, waits for them, and re-layouts: 10.2 us -> 0.01 us
where the time goes in v2:
time: 33.3 us; the launch traced here: 33.1 us
  Pallas kernels  32.4 us (97%)
  between operations  0.67 us (2%)
    pallas_call x1, Pallas kernels, flame(): pl.pallas_call(functools.partial(flame_kernel, grid_x, grid_y), out_shape...  31.4 us
    pallas_call x1, Pallas kernels, flame(): pl.pallas_call(final_kernel, out_shape=(shaped((nspec, columns, depth)),...  1.01 us

profile of v2, /device:TPU:0, one launch (start us, length us, event | category | flops | bytes accessed | tf_op | source)
XLA Modules:
  0.0 33.1 jit_solution(6002516025983588422)
XLA Ops:
  0.6 0.0 copy-start
  0.6 0.0 copy-start.1
  0.7 31.4 %flame.1 = (f32[9,64,128]{2,1,0:T(8,128)S(1)}, f32[5,64,128]{2,1,0:T(8,128)S(1)}, f32[32,8,128]{2,1,0:T(8,128)S(1)}) custom-call(f32[9,64,128]{2,1,0:T(8,128)} %bitcast.10, f32[5,64,128]{2,1,0:T(8,128)} %bitcast.11, s32[8,8]{1,0:T(8,128)} %kinds_hbm.1, f32[14]{0:T(128)} %diffusivity_hbm.1, f32[9,19]{1,0:T(8,128)} %bitcast.12, f32[9,19]{1,0:T(8,128)} %bitcast.13, ...), custom_call_target="tpu_custom_call" | custom-call | tf_op jit(solution)/shard_map/flame/pallas_call | solution.py:753
  32.1 0.0 copy-done
  32.1 0.0 copy-done.1
  32.1 1.0 %final.1 = (f32[9,64,128]{2,1,0:T(8,128)}, f32[5,64,128]{2,1,0:T(8,128)}) custom-call(bf16[256,384]{1,0:T(8,128)(2,1)S(1)} %copy-done.1, bf16[256,384]{1,0:T(8,128)(2,1)S(1)} %copy-done, f32[9,64,128]{2,1,0:T(8,128)S(1)} %get-tuple-element.7.species_in, f32[5,64,128]{2,1,0:T(8,128)S(1)} %get-tuple-element.8.flow_in, f32[32,8,128]{2,1,0:T(8,128)S(1)} %get-tuple-element.9.gathered), custom_call_target="tpu_custom_call" | custom-call | tf_op jit(solution)/shard_map/final/pallas_call | solution.py:762
Async XLA Ops:
  0.6 31.5 %copy-start = (bf16[256,384]{1,0:T(8,128)(2,1)S(1)}, bf16[256,384]{1,0:T(8,128)(2,1)}, u32[]{:S(2)}) copy-start(bf16[256,384]{1,0:T(8,128)(2,1)} %constant.11.clone.back_l) | copy-start | bytes 589828
  0.6 31.5 %copy-start.1 = (bf16[256,384]{1,0:T(8,128)(2,1)S(1)}, bf16[256,384]{1,0:T(8,128)(2,1)}, u32[]{:S(2)}) copy-start(bf16[256,384]{1,0:T(8,128)(2,1)} %constant.10.clone.back_h) | copy-start | bytes 589828
